TPU v7x, 32 devices: a whole 2x2x4 slice. The times are simulated.
32 devices in a mesh: seq: 8 (over z, x), tp: 4 (over y, core).
Axes of the slice: x: 2, y: 2, z: 4, core: 2. Of those that a mesh axis runs over, the one named last changes fastest.
Arguments:
- inputs: bfloat16 [2, 2048, 2048], P(None, 'seq'), may hold values from -6 to 6
- cotangent: bfloat16 [2, 2048, 2048], P(None, 'seq'), may hold values from -6 to 6
- attn_gain: bfloat16 [2048], P('seq'), may hold values from 0.5 to 1.5
- w_query: bfloat16 [2048, 2048], P('seq', 'tp'), may hold values from -0.125 to 0.125
- w_key: bfloat16 [2048, 2048], P('seq', 'tp'), may hold values from -0.125 to 0.125
- w_value: bfloat16 [2048, 3456], P('seq', 'tp'), may hold values from -0.125 to 0.125
- w_gate: bfloat16 [2048, 3456], P('seq', 'tp'), may hold values from -0.125 to 0.125
- w_out: bfloat16 [3456, 2048], P('tp', 'seq'), may hold values from -0.15625 to 0.15625
- ffn_gain: bfloat16 [2048], P('seq'), may hold values from 0.5 to 1.5
- w_glu: bfloat16 [2048, 3456], P('seq', 'tp'), may hold values from -0.125 to 0.125
- w_up: bfloat16 [2048, 3456], P('seq', 'tp'), may hold values from -0.125 to 0.125
- w_down: bfloat16 [3456, 2048], P('tp', 'seq'), may hold values from -0.15625 to 0.15625
- decay_rate: float32 [8], P('tp'), may hold values from 0 to 0.032, as said below
Outputs:
- outputs: bfloat16 [2, 2048, 2048], P(None, 'seq')
- input_grad: float32 [2, 2048, 2048], P(None, 'seq')
- attngain_grad: float32 [2048], P('seq')
- query_grad: float32 [2048, 2048], P('seq', 'tp')
- key_grad: float32 [2048, 2048], P('seq', 'tp')
- value_grad: float32 [2048, 3456], P('seq', 'tp')
- gate_grad: float32 [2048, 3456], P('seq', 'tp')
- out_grad: float32 [3456, 2048], P('tp', 'seq')
- ffngain_grad: float32 [2048], P('seq')
- glu_grad: float32 [2048, 3456], P('seq', 'tp')
- up_grad: float32 [2048, 3456], P('seq', 'tp')
- down_grad: float32 [3456, 2048], P('tp', 'seq')
Inputs may be any that keep to these rules, and one draw needn't show every extreme that they name: `decay_rate`: each head's decay rate; positive.
All inputs are finite; a program needn't handle non-finite values.
Results may differ from a plain program's by a relative error of at most 0.03.
Values may be sent and summed in bfloat16 or wider, within the bound.
A program may use at most 256 MiB of HBM per device.

v0:
```python
import math

import jax
import jax.numpy as jnp
from jax import lax
from jax.sharding import PartitionSpec as P

KEY = 256
VAL = 432


EPS_LAYER = 1e-05
EPS_GROUP = 1e-06
MAXIMAL_ACCURACY = lax.Precision.HIGHEST


def passed_along(block, axis, distance):
    devices = range(lax.axis_size(axis))
    route = [(i - distance, i) for i in devices if i - distance in devices]
    return lax.ppermute(block, axis, route)


def normalize(values, epsilon):
    average = jnp.mean(values, axis=-1, keepdims=True)
    centred = values - average
    inv_std = lax.rsqrt(jnp.mean(centred * centred, axis=-1, keepdims=True) + epsilon)
    return (centred * inv_std, inv_std)


def normalize_back(upstream, normed, inv_std):
    return inv_std * (
        upstream
        - jnp.mean(upstream, axis=-1, keepdims=True)
        - normed * jnp.mean(upstream * normed, axis=-1, keepdims=True)
    )


def swish_parts(values):
    sigmoid = jax.nn.sigmoid(values)
    return (values * sigmoid, sigmoid * (1.0 + values * (1.0 - sigmoid)))


def rotary_tables(positions, width):
    half_width = width // 2
    fraction = jnp.arange(half_width, dtype=jnp.float32) / max(half_width - 1, 1)
    frequency = jnp.power(10000.0, -fraction)
    angles = positions[:, None] * frequency[None, :]
    cosine = jnp.concatenate([jnp.cos(angles), jnp.cos(angles)], axis=-1)[:, None, :]
    sine_table = jnp.concatenate([jnp.sin(angles), jnp.sin(angles)], axis=-1)[:, None, :]
    return (cosine, sine_table)


def rotate(values, cosine, sine_table):
    half_width = values.shape[-1] // 2
    turned = jnp.concatenate([-values[..., half_width:], values[..., :half_width]], axis=-1)
    return values * cosine + turned * sine_table


def rotate_back(upstream, cosine, sine_table):
    half_width = upstream.shape[-1] // 2
    scaled = upstream * sine_table
    turned = jnp.concatenate([scaled[..., half_width:], -scaled[..., :half_width]], axis=-1)
    return upstream * cosine + turned


def decay_tables(rates, length):
    offsets = jnp.arange(length, dtype=jnp.float32)
    distance = offsets[:, None] - offsets[None, :]
    decay_mask = jnp.where(
        distance[None] >= 0.0,
        jnp.exp(-rates[:, None, None] * jnp.maximum(distance, 0.0)[None]),
        0.0,
    )
    leading_decay = jnp.exp(-rates[None, :] * (offsets[:, None] + 1.0))
    trailing_decay = jnp.exp(-rates[None, :] * (length - 1.0 - offsets[:, None]))
    return (decay_mask, leading_decay, trailing_decay)


def block_summary(key_rotated, value_matrix_rows, trailing_decay):
    return jnp.einsum(
        "ysu,ysb->sub",
        key_rotated.astype(jnp.float32) * trailing_decay[:, :, None],
        value_matrix_rows.astype(jnp.float32),
        precision=MAXIMAL_ACCURACY,
    )


def block_weights(query_rotated, key_rotated, decay_mask):
    scores = jnp.einsum(
        "ihk,jhk->hij", query_rotated, key_rotated, preferred_element_type=jnp.float32
    )
    return (scores * decay_mask).astype(jnp.bfloat16)


def block_output(
    query_rotated, key_rotated, value_matrix_rows, incoming_state, decay_mask, leading_decay
):
    layer_weights = block_weights(query_rotated, key_rotated, decay_mask)
    inner = jnp.einsum(
        "hij,jhv->ihv", layer_weights, value_matrix_rows, preferred_element_type=jnp.float32
    )
    carried_state = jnp.einsum(
        "jnq,nqs->jns",
        query_rotated.astype(jnp.float32) * leading_decay[:, :, None],
        incoming_state,
        precision=MAXIMAL_ACCURACY,
    )
    return inner + carried_state


def state_grad_own(query_rotated, output_gradient, leading_decay):
    return jnp.einsum(
        "pxa,pxb->xab",
        query_rotated.astype(jnp.float32) * leading_decay[:, :, None],
        output_gradient.astype(jnp.float32),
        precision=MAXIMAL_ACCURACY,
    )


def block_backward(
    query_rotated,
    key_rotated,
    value_matrix_rows,
    incoming_state,
    state_gradient,
    output_gradient,
    decay_mask,
    leading_decay,
    trailing_decay,
):
    weight_gradients = (
        jnp.einsum(
            "ihv,jhv->hij", output_gradient, value_matrix_rows, preferred_element_type=jnp.float32
        )
        * decay_mask
    ).astype(jnp.bfloat16)
    layer_weights = block_weights(query_rotated, key_rotated, decay_mask)
    query_gradient = jnp.einsum(
        "pzg,gpe->zpe", weight_gradients, key_rotated, preferred_element_type=jnp.float32
    ) + leading_decay[:, :, None] * jnp.einsum(
        "wcr,cdr->wcd",
        output_gradient.astype(jnp.float32),
        incoming_state,
        precision=MAXIMAL_ACCURACY,
    )
    key_gradient = jnp.einsum(
        "zun,uzf->nzf", weight_gradients, query_rotated, preferred_element_type=jnp.float32
    ) + trailing_decay[:, :, None] * jnp.einsum(
        "crp,rnp->crn",
        value_matrix_rows.astype(jnp.float32),
        state_gradient,
        precision=MAXIMAL_ACCURACY,
    )
    value_gradient = jnp.einsum(
        "lpb,plz->blz", layer_weights, output_gradient, preferred_element_type=jnp.float32
    ) + trailing_decay[:, :, None] * jnp.einsum(
        "zmf,mfn->zmn", key_rotated.astype(jnp.float32), state_gradient, precision=MAXIMAL_ACCURACY
    )
    return (query_gradient, key_gradient, value_gradient)


def carry_states(whole_decay, summary):

    def advance(turn_index, carried_state):
        return passed_along(whole_decay * carried_state + summary, "seq", 1)

    return lax.fori_loop(0, lax.axis_size("seq") - 1, advance, jnp.zeros_like(summary))


def carry_back(whole_decay, own_grad):

    def retreat(turn_index, carried_state):
        return passed_along(whole_decay * carried_state + own_grad, "seq", -1)

    return lax.fori_loop(0, lax.axis_size("seq") - 1, retreat, jnp.zeros_like(own_grad))


def on_device(
    inputs,
    cotangent,
    attn_gain,
    w_query,
    w_key,
    w_value,
    w_gate,
    w_out,
    ffn_gain,
    w_glu,
    w_up,
    w_down,
    decay_rate,
):
    seq_count, tok_rows, model_width = inputs.shape
    row_count = seq_count * tok_rows
    local_heads = decay_rate.shape[0]
    gathered = (
        lax.all_gather(w_query, "seq", axis=0, tiled=True),
        lax.all_gather(w_key, "seq", axis=0, tiled=True),
        lax.all_gather(w_value, "seq", axis=0, tiled=True),
        lax.all_gather(w_gate, "seq", axis=0, tiled=True),
        lax.all_gather(w_out, "seq", axis=1, tiled=True),
        lax.all_gather(w_glu, "seq", axis=0, tiled=True),
        lax.all_gather(w_up, "seq", axis=0, tiled=True),
        lax.all_gather(w_down, "seq", axis=1, tiled=True),
        lax.all_gather(attn_gain, "seq", axis=0, tiled=True),
        lax.all_gather(ffn_gain, "seq", axis=0, tiled=True),
    )
    (
        full_query,
        full_key,
        full_value,
        full_gate,
        full_out,
        full_glu,
        full_up,
        full_down,
        full_attn_gain,
        full_ffn_gain,
    ) = gathered
    residual = inputs.astype(jnp.float32).reshape(row_count, model_width)
    normed_one, inv_one = normalize(residual, EPS_LAYER)
    attn_in = (normed_one * full_attn_gain.astype(jnp.float32)).astype(jnp.bfloat16)
    query_lin = jnp.dot(attn_in, full_query, preferred_element_type=jnp.float32)
    key_lin = jnp.dot(attn_in, full_key, preferred_element_type=jnp.float32)
    value_lin = jnp.dot(attn_in, full_value, preferred_element_type=jnp.float32)
    gate_lin = jnp.dot(attn_in, full_gate, preferred_element_type=jnp.float32)
    offset = (lax.axis_index("seq") * tok_rows).astype(jnp.float32)
    positions = offset + jnp.arange(tok_rows, dtype=jnp.float32)
    cosine, sine_table = rotary_tables(positions, KEY)
    key_scale = 1.0 / math.sqrt(KEY)
    query_rotated = rotate(
        query_lin.reshape(seq_count, tok_rows, local_heads, KEY), cosine, sine_table
    ).astype(jnp.bfloat16)
    key_rotated = (
        rotate(key_lin.reshape(seq_count, tok_rows, local_heads, KEY), cosine, sine_table)
        * key_scale
    ).astype(jnp.bfloat16)
    value_matrix_rows = value_lin.reshape(seq_count, tok_rows, local_heads, VAL).astype(
        jnp.bfloat16
    )
    decay_mask, leading_decay, trailing_decay = decay_tables(decay_rate, tok_rows)
    whole_decay = jnp.exp(-decay_rate * tok_rows)[:, None, None]
    summary = jax.vmap(block_summary, in_axes=(0, 0, None))(
        key_rotated, value_matrix_rows, trailing_decay
    )
    incoming_state = carry_states(whole_decay, summary)
    retained = jax.vmap(block_output, in_axes=(0, 0, 0, 0, None, None))(
        query_rotated, key_rotated, value_matrix_rows, incoming_state, decay_mask, leading_decay
    )
    group_normed, group_inv = normalize(retained, EPS_GROUP)
    gate_act, gate_slope = swish_parts(gate_lin)
    group_flat = group_normed.reshape(row_count, local_heads * VAL)
    mixed = (gate_act * group_flat).astype(jnp.bfloat16)
    attn_out = lax.psum(jnp.dot(mixed, full_out, preferred_element_type=jnp.float32), "tp")
    middle = residual + attn_out
    normed_two, inv_two = normalize(middle, EPS_LAYER)
    ffn_in = (normed_two * full_ffn_gain.astype(jnp.float32)).astype(jnp.bfloat16)
    glu_lin = jnp.dot(ffn_in, full_glu, preferred_element_type=jnp.float32)
    up_lin = jnp.dot(ffn_in, full_up, preferred_element_type=jnp.float32)
    glu_act, glu_slope = swish_parts(glu_lin)
    hidden = (glu_act * up_lin).astype(jnp.bfloat16)
    ffn_out = lax.psum(jnp.dot(hidden, full_down, preferred_element_type=jnp.float32), "tp")
    final = middle + ffn_out
    outputs = final.astype(jnp.bfloat16).reshape(seq_count, tok_rows, model_width)
    back_weights = (
        lax.all_gather(w_query, "seq", axis=0, tiled=True),
        lax.all_gather(w_key, "seq", axis=0, tiled=True),
        lax.all_gather(w_value, "seq", axis=0, tiled=True),
        lax.all_gather(w_gate, "seq", axis=0, tiled=True),
        lax.all_gather(w_out, "seq", axis=1, tiled=True),
        lax.all_gather(w_glu, "seq", axis=0, tiled=True),
        lax.all_gather(w_up, "seq", axis=0, tiled=True),
        lax.all_gather(w_down, "seq", axis=1, tiled=True),
        lax.all_gather(attn_gain, "seq", axis=0, tiled=True),
        lax.all_gather(ffn_gain, "seq", axis=0, tiled=True),
    )
    (
        back_query,
        back_key,
        back_value,
        back_gate,
        back_out,
        back_glu,
        back_up,
        back_down,
        back_attn_gain,
        back_ffn_gain,
    ) = back_weights
    cot_rows = cotangent.reshape(row_count, model_width)
    down_grad = jnp.dot(hidden.T, cot_rows, preferred_element_type=jnp.float32)
    grad_hidden = jnp.dot(cot_rows, back_down.T, preferred_element_type=jnp.float32)
    grad_glu = (grad_hidden * up_lin * glu_slope).astype(jnp.bfloat16)
    grad_up = (grad_hidden * glu_act).astype(jnp.bfloat16)
    glu_grad = jnp.dot(ffn_in.T, grad_glu, preferred_element_type=jnp.float32)
    up_grad = jnp.dot(ffn_in.T, grad_up, preferred_element_type=jnp.float32)
    grad_ffn_in = lax.psum(
        jnp.dot(grad_glu, back_glu.T, preferred_element_type=jnp.float32)
        + jnp.dot(grad_up, back_up.T, preferred_element_type=jnp.float32),
        "tp",
    )
    ffngain_grad = jnp.sum(grad_ffn_in * normed_two, axis=0)
    grad_middle = cot_rows.astype(jnp.float32) + normalize_back(
        grad_ffn_in * back_ffn_gain.astype(jnp.float32), normed_two, inv_two
    )
    grad_middle_bf = grad_middle.astype(jnp.bfloat16)
    out_grad = jnp.dot(mixed.T, grad_middle_bf, preferred_element_type=jnp.float32)
    grad_mixed = jnp.dot(grad_middle_bf, back_out.T, preferred_element_type=jnp.float32)
    grad_gate = (grad_mixed * group_flat * gate_slope).astype(jnp.bfloat16)
    grad_group = (grad_mixed * gate_act).reshape(seq_count, tok_rows, local_heads, VAL)
    grad_retained = normalize_back(grad_group, group_normed, group_inv).astype(jnp.bfloat16)
    own_grad = jax.vmap(state_grad_own, in_axes=(0, 0, None))(
        query_rotated, grad_retained, leading_decay
    )
    state_gradient = carry_back(whole_decay, own_grad)
    grad_qrot, grad_krot, grad_vrows = jax.vmap(
        block_backward, in_axes=(0, 0, 0, 0, 0, 0, None, None, None)
    )(
        query_rotated,
        key_rotated,
        value_matrix_rows,
        incoming_state,
        state_gradient,
        grad_retained,
        decay_mask,
        leading_decay,
        trailing_decay,
    )
    query_gradient = (
        rotate_back(grad_qrot, cosine, sine_table)
        .reshape(row_count, local_heads * KEY)
        .astype(jnp.bfloat16)
    )
    key_gradient = (
        (rotate_back(grad_krot, cosine, sine_table) * key_scale)
        .reshape(row_count, local_heads * KEY)
        .astype(jnp.bfloat16)
    )
    value_gradient = grad_vrows.reshape(row_count, local_heads * VAL).astype(jnp.bfloat16)
    query_grad = jnp.dot(attn_in.T, query_gradient, preferred_element_type=jnp.float32)
    key_grad = jnp.dot(attn_in.T, key_gradient, preferred_element_type=jnp.float32)
    value_grad = jnp.dot(attn_in.T, value_gradient, preferred_element_type=jnp.float32)
    gate_grad = jnp.dot(attn_in.T, grad_gate, preferred_element_type=jnp.float32)
    partial_in = (
        jnp.dot(query_gradient, back_query.T, preferred_element_type=jnp.float32)
        + jnp.dot(key_gradient, back_key.T, preferred_element_type=jnp.float32)
        + jnp.dot(value_gradient, back_value.T, preferred_element_type=jnp.float32)
        + jnp.dot(grad_gate, back_gate.T, preferred_element_type=jnp.float32)
    )
    grad_attn_in = lax.psum(partial_in, "tp")
    attngain_grad = jnp.sum(grad_attn_in * normed_one, axis=0)
    input_grad = grad_middle + normalize_back(
        grad_attn_in * back_attn_gain.astype(jnp.float32), normed_one, inv_one
    )
    input_out = input_grad.reshape(seq_count, tok_rows, model_width)
    reduced = (
        lax.psum_scatter(query_grad, "seq", scatter_dimension=0, tiled=True),
        lax.psum_scatter(key_grad, "seq", scatter_dimension=0, tiled=True),
        lax.psum_scatter(value_grad, "seq", scatter_dimension=0, tiled=True),
        lax.psum_scatter(gate_grad, "seq", scatter_dimension=0, tiled=True),
        lax.psum_scatter(out_grad, "seq", scatter_dimension=1, tiled=True),
        lax.psum_scatter(glu_grad, "seq", scatter_dimension=0, tiled=True),
        lax.psum_scatter(up_grad, "seq", scatter_dimension=0, tiled=True),
        lax.psum_scatter(down_grad, "seq", scatter_dimension=1, tiled=True),
        lax.psum_scatter(attngain_grad, "seq", scatter_dimension=0, tiled=True),
        lax.psum_scatter(ffngain_grad, "seq", scatter_dimension=0, tiled=True),
    )
    return (
        outputs,
        input_out,
        reduced[8],
        reduced[0],
        reduced[1],
        reduced[2],
        reduced[3],
        reduced[4],
        reduced[9],
        reduced[5],
        reduced[6],
        reduced[7],
    )


def solution(mesh):
    return jax.shard_map(
        on_device,
        mesh=mesh,
        in_specs=(
            P(None, "seq", None),
            P(None, "seq", None),
            P("seq"),
            P("seq", "tp"),
            P("seq", "tp"),
            P("seq", "tp"),
            P("seq", "tp"),
            P("tp", "seq"),
            P("seq"),
            P("seq", "tp"),
            P("seq", "tp"),
            P("tp", "seq"),
            P("tp"),
        ),
        out_specs=(
            P(None, "seq", None),
            P(None, "seq", None),
            P("seq"),
            P("seq", "tp"),
            P("seq", "tp"),
            P("seq", "tp"),
            P("seq", "tp"),
            P("tp", "seq"),
            P("seq"),
            P("seq", "tp"),
            P("seq", "tp"),
            P("tp", "seq"),
        ),
        check_vma=False,
    )
```

profile of v0, /device:TPU:0, one launch (start us, length us, event | category | flops | bytes accessed | tf_op | source)
XLA Modules:
  0.0 2463.4 jit_solution(17136700813776060130)
XLA Ops:
  66.0 45.9 %all-gather.15.cloned.1.call-done = bf16[2048,512]{1,0:T(8,128)(2,1)} async-done(((bf16[256,512]{1,0:T(8,128)(2,1)}), bf16[2048,512]{1,0:T(8,128)(2,1)}) %all-gather.15.cloned.1.call-update) | async-done | bytes 2097168 | tf_op jit(solution)/shard_map/all_gather | solution.py:197
  122.3 57.4 %all-gather.13.cloned.1.call-done = bf16[2048,864]{0,1:T(8,128)(2,1)} async-done(((bf16[256,864]{0,1:T(8,128)(2,1)}), bf16[2048,864]{0,1:T(8,128)(2,1)}) %all-gather.13.cloned.1.call-update) | async-done | bytes 3538960 | tf_op jit(solution)/shard_map/all_gather | solution.py:199
  186.6 372.9 %while.20 = (s32[]{:T(128)}, f32[2,2,256,432]{2,3,1,0:T(8,128)S(1)}, f32[2]{0:T(128)S(1)}, f32[2,2,256,432]{2,3,1,0:T(8,128)S(1)}, s32[]{:T(128)}) while((s32[]{:T(128)}, f32[2,2,256,432]{2,3,1,0:T(8,128)S(1)}, f32[2]{0:T(128)S(1)}, f32[2,2,256,432]{2,3,1,0:T(8,128)S(1)}, s32[]{:T(128)}) %tuple.65), condition=%wide.region_3.4_spmd, body=%wide.region_2.3_spmd.sunk | while | flops 884738 | bytes 12386413 | solution.py:167
  191.6 49.0 %collective-permute-done = f32[2,2,256,432]{2,3,1,0:T(8,128)S(1)} collective-permute-done((f32[2,2,256,432]{2,3,1,0:T(8,128)}, f32[2,2,256,432]{2,3,1,0:T(8,128)S(1)}, u32[]{:S(2)}, u32[]{:S(2)}) %collective-permute-start) | collective-permute-done | bytes 1769504 | tf_op jit(solution)/shard_map/while/body/eval_jaxpr/ppermute | solution.py:20
  265.3 42.4 %collective-permute-done = f32[2,2,256,432]{2,3,1,0:T(8,128)S(1)} collective-permute-done((f32[2,2,256,432]{2,3,1,0:T(8,128)}, f32[2,2,256,432]{2,3,1,0:T(8,128)S(1)}, u32[]{:S(2)}, u32[]{:S(2)}) %collective-permute-start) | collective-permute-done | bytes 1769504 | tf_op jit(solution)/shard_map/while/body/eval_jaxpr/ppermute | solution.py:20
  327.7 50.1 %collective-permute-done = f32[2,2,256,432]{2,3,1,0:T(8,128)S(1)} collective-permute-done((f32[2,2,256,432]{2,3,1,0:T(8,128)}, f32[2,2,256,432]{2,3,1,0:T(8,128)S(1)}, u32[]{:S(2)}, u32[]{:S(2)}) %collective-permute-start) | collective-permute-done | bytes 1769504 | tf_op jit(solution)/shard_map/while/body/eval_jaxpr/ppermute | solution.py:20
  393.1 37.7 %collective-permute-done = f32[2,2,256,432]{2,3,1,0:T(8,128)S(1)} collective-permute-done((f32[2,2,256,432]{2,3,1,0:T(8,128)}, f32[2,2,256,432]{2,3,1,0:T(8,128)S(1)}, u32[]{:S(2)}, u32[]{:S(2)}) %collective-permute-start) | collective-permute-done | bytes 1769504 | tf_op jit(solution)/shard_map/while/body/eval_jaxpr/ppermute | solution.py:20
  437.6 36.8 %collective-permute-done = f32[2,2,256,432]{2,3,1,0:T(8,128)S(1)} collective-permute-done((f32[2,2,256,432]{2,3,1,0:T(8,128)}, f32[2,2,256,432]{2,3,1,0:T(8,128)S(1)}, u32[]{:S(2)}, u32[]{:S(2)}) %collective-permute-start) | collective-permute-done | bytes 1769504 | tf_op jit(solution)/shard_map/while/body/eval_jaxpr/ppermute | solution.py:20
  481.3 36.0 %collective-permute-done = f32[2,2,256,432]{2,3,1,0:T(8,128)S(1)} collective-permute-done((f32[2,2,256,432]{2,3,1,0:T(8,128)}, f32[2,2,256,432]{2,3,1,0:T(8,128)S(1)}, u32[]{:S(2)}, u32[]{:S(2)}) %collective-permute-start) | collective-permute-done | bytes 1769504 | tf_op jit(solution)/shard_map/while/body/eval_jaxpr/ppermute | solution.py:20
  601.9 65.1 %all-reduce.8.cloned.1.call-done = f32[512,2048]{1,0:T(8,128)} async-done(((f32[512,2048]{1,0:T(8,128)}), f32[512,2048]{1,0:T(8,128)}) %all-reduce.8.cloned.1.call-update) | async-done | bytes 4194320 | tf_op jit(solution)/shard_map/psum | solution.py:254
  674.4 62.0 %all-gather.21.cloned.1.call-done = bf16[2048,864]{0,1:T(8,128)(2,1)} async-done(((bf16[256,864]{0,1:T(8,128)(2,1)}), bf16[2048,864]{0,1:T(8,128)(2,1)}) %all-gather.21.cloned.1.call-update) | async-done | bytes 3538960 | tf_op jit(solution)/shard_map/all_gather | solution.py:202
  742.2 61.6 %all-gather.23.cloned.1.call-done = bf16[2048,864]{0,1:T(8,128)(2,1)} async-done(((bf16[256,864]{0,1:T(8,128)(2,1)}), bf16[2048,864]{0,1:T(8,128)(2,1)}) %all-gather.23.cloned.1.call-update) | async-done | bytes 3538960 | tf_op jit(solution)/shard_map/all_gather | solution.py:203
  809.7 61.5 %all-gather.25.cloned.1.call-done = bf16[864,2048]{1,0:T(8,128)(2,1)} async-done(((bf16[864,256]{1,0:T(8,128)(2,1)}), bf16[864,2048]{1,0:T(8,128)(2,1)}) %all-gather.25.cloned.1.call-update) | async-done | bytes 3538960 | tf_op jit(solution)/shard_map/all_gather | solution.py:204
  892.6 77.0 %all-reduce.10.cloned.1.call-done = f32[512,2048]{1,0:T(8,128)} async-done(((f32[512,2048]{1,0:T(8,128)}), f32[512,2048]{1,0:T(8,128)}) %all-reduce.10.cloned.1.call-update) | async-done | bytes 4194320 | tf_op jit(solution)/shard_map/psum | solution.py:296
  1001.0 293.1 %while.21 = (s32[]{:T(128)}, f32[2,2,256,432]{2,3,1,0:T(8,128)S(1)}, f32[2]{0:T(128)S(1)}, f32[2,2,256,432]{2,3,1,0:T(8,128)S(1)}, s32[]{:T(128)}) while((s32[]{:T(128)}, f32[2,2,256,432]{2,3,1,0:T(8,128)S(1)}, f32[2]{0:T(128)S(1)}, f32[2,2,256,432]{2,3,1,0:T(8,128)S(1)}, s32[]{:T(128)}) %tuple.110), condition=%wide.region_16.17_spmd, body=%wide.region_15.16_spmd.sunk | while | flops 884738 | bytes 12386413 | solution.py:175
  1003.9 40.8 %collective-permute-done.1 = f32[2,2,256,432]{2,3,1,0:T(8,128)S(1)} collective-permute-done((f32[2,2,256,432]{2,3,1,0:T(8,128)}, f32[2,2,256,432]{2,3,1,0:T(8,128)S(1)}, u32[]{:S(2)}, u32[]{:S(2)}) %collective-permute-start.1) | collective-permute-done | bytes 1769504 | tf_op jit(solution)/shard_map/while/body/eval_jaxpr/ppermute | solution.py:20
  1047.5 40.6 %collective-permute-done.1 = f32[2,2,256,432]{2,3,1,0:T(8,128)S(1)} collective-permute-done((f32[2,2,256,432]{2,3,1,0:T(8,128)}, f32[2,2,256,432]{2,3,1,0:T(8,128)S(1)}, u32[]{:S(2)}, u32[]{:S(2)}) %collective-permute-start.1) | collective-permute-done | bytes 1769504 | tf_op jit(solution)/shard_map/while/body/eval_jaxpr/ppermute | solution.py:20
  1091.0 40.0 %collective-permute-done.1 = f32[2,2,256,432]{2,3,1,0:T(8,128)S(1)} collective-permute-done((f32[2,2,256,432]{2,3,1,0:T(8,128)}, f32[2,2,256,432]{2,3,1,0:T(8,128)S(1)}, u32[]{:S(2)}, u32[]{:S(2)}) %collective-permute-start.1) | collective-permute-done | bytes 1769504 | tf_op jit(solution)/shard_map/while/body/eval_jaxpr/ppermute | solution.py:20
  1133.8 39.2 %collective-permute-done.1 = f32[2,2,256,432]{2,3,1,0:T(8,128)S(1)} collective-permute-done((f32[2,2,256,432]{2,3,1,0:T(8,128)}, f32[2,2,256,432]{2,3,1,0:T(8,128)S(1)}, u32[]{:S(2)}, u32[]{:S(2)}) %collective-permute-start.1) | collective-permute-done | bytes 1769504 | tf_op jit(solution)/shard_map/while/body/eval_jaxpr/ppermute | solution.py:20
  1175.8 38.3 %collective-permute-done.1 = f32[2,2,256,432]{2,3,1,0:T(8,128)S(1)} collective-permute-done((f32[2,2,256,432]{2,3,1,0:T(8,128)}, f32[2,2,256,432]{2,3,1,0:T(8,128)S(1)}, u32[]{:S(2)}, u32[]{:S(2)}) %collective-permute-start.1) | collective-permute-done | bytes 1769504 | tf_op jit(solution)/shard_map/while/body/eval_jaxpr/ppermute | solution.py:20
  1217.0 37.5 %collective-permute-done.1 = f32[2,2,256,432]{2,3,1,0:T(8,128)S(1)} collective-permute-done((f32[2,2,256,432]{2,3,1,0:T(8,128)}, f32[2,2,256,432]{2,3,1,0:T(8,128)S(1)}, u32[]{:S(2)}, u32[]{:S(2)}) %collective-permute-start.1) | collective-permute-done | bytes 1769504 | tf_op jit(solution)/shard_map/while/body/eval_jaxpr/ppermute | solution.py:20
  1257.3 36.6 %collective-permute-done.1 = f32[2,2,256,432]{2,3,1,0:T(8,128)S(1)} collective-permute-done((f32[2,2,256,432]{2,3,1,0:T(8,128)}, f32[2,2,256,432]{2,3,1,0:T(8,128)S(1)}, u32[]{:S(2)}, u32[]{:S(2)}) %collective-permute-start.1) | collective-permute-done | bytes 1769504 | tf_op jit(solution)/shard_map/while/body/eval_jaxpr/ppermute | solution.py:20
  1372.8 101.0 %all-reduce.12.cloned.1.call-done = (f32[512,2048]{1,0:T(8,128)}, f32[512,2048]{1,0:T(8,128)}) async-done(((f32[512,2048]{1,0:T(8,128)}, f32[512,2048]{1,0:T(8,128)}), (f32[512,2048]{1,0:T(8,128)}, f32[512,2048]{1,0:T(8,128)})) %all-reduce.12.cloned.1.call-update) | async-done | bytes 8388624 | tf_op jit(solution)/shard_map/psum | solution.py:262
  1477.3 38.5 %all-reduce.2 = (f32[2048]{0:T(1024)S(1)}, f32[2048]{0:T(1024)S(1)}) all-reduce(f32[2048]{0:T(1024)S(1)} %get-tuple-element.76, f32[2048]{0:T(1024)S(1)} %copy-done.58), channel_id=2, replica_groups=mesh['seq'=8,'tp'=4] {'seq'}, use_global_device_ids=true, to_apply=%region_21.22.clone | all-reduce | flops 4096 | bytes 32768
  1526.9 39.8 %reduce-scatter.11.cloned.1.call-done = f32[256,512]{1,0:T(8,128)} async-done(((f32[2048,512]{1,0:T(8,128)}), f32[256,512]{1,0:T(8,128)}) %reduce-scatter.11.cloned.1.call-update) | async-done | bytes 524304 | tf_op jit(solution)/shard_map/reduce_scatter | solution.py:357
  1566.8 92.2 %reduce-scatter.9.cloned.1.call-done = f32[256,512]{1,0:T(8,128)} async-done(((f32[2048,512]{1,0:T(8,128)}), f32[256,512]{1,0:T(8,128)}) %reduce-scatter.9.cloned.1.call-update) | async-done | bytes 524304 | tf_op jit(solution)/shard_map/reduce_scatter | solution.py:356
  1658.9 133.3 %reduce-scatter.19.cloned.1.call-done = f32[256,864]{0,1:T(8,128)} async-done(((f32[2048,864]{0,1:T(8,128)}), f32[256,864]{0,1:T(8,128)}) %reduce-scatter.19.cloned.1.call-update) | async-done | bytes 884752 | tf_op jit(solution)/shard_map/reduce_scatter | solution.py:361
  1792.3 132.8 %reduce-scatter.21.cloned.1.call-done = f32[256,864]{0,1:T(8,128)} async-done(((f32[2048,864]{0,1:T(8,128)}), f32[256,864]{0,1:T(8,128)}) %reduce-scatter.21.cloned.1.call-update) | async-done | bytes 884752 | tf_op jit(solution)/shard_map/reduce_scatter | solution.py:362
  1925.1 132.9 %reduce-scatter.23.cloned.1.call-done = f32[864,256]{1,0:T(8,128)} async-done(((f32[864,2048]{1,0:T(8,128)}), f32[864,256]{1,0:T(8,128)}) %reduce-scatter.23.cloned.1.call-update) | async-done | bytes 884752 | tf_op jit(solution)/shard_map/reduce_scatter | solution.py:363
  2058.0 132.8 %reduce-scatter.17.cloned.1.call-done = f32[864,256]{1,0:T(8,128)} async-done(((f32[864,2048]{1,0:T(8,128)}), f32[864,256]{1,0:T(8,128)}) %reduce-scatter.17.cloned.1.call-update) | async-done | bytes 884752 | tf_op jit(solution)/shard_map/reduce_scatter | solution.py:360
  2190.8 132.8 %reduce-scatter.13.cloned.1.call-done = f32[256,864]{0,1:T(8,128)} async-done(((f32[2048,864]{0,1:T(8,128)}), f32[256,864]{0,1:T(8,128)}) %reduce-scatter.13.cloned.1.call-update) | async-done | bytes 884752 | tf_op jit(solution)/shard_map/reduce_scatter | solution.py:358
  2323.7 133.0 %reduce-scatter.15.cloned.1.call-done = f32[256,864]{0,1:T(8,128)} async-done(((f32[2048,864]{0,1:T(8,128)}), f32[256,864]{0,1:T(8,128)}) %reduce-scatter.15.cloned.1.call-update) | async-done | bytes 884752 | tf_op jit(solution)/shard_map/reduce_scatter | solution.py:359
  (311 shorter events, 422.4 us)
Async XLA Ops:
  7.2 54.9 %all-gather.17.cloned.1.call-start = ((), (), s32[]{:S(2)}) async-start(), calls=%async_computation.11 | async-start | bytes 2359296 | tf_op jit(solution)/shard_map/all_gather | solution.py:198
  7.9 103.9 %all-gather.15.cloned.1.call-start = ((), (), s32[]{:S(2)}) async-start(), calls=%async_computation.10 | async-start | bytes 2359296 | tf_op jit(solution)/shard_map/all_gather | solution.py:197
  8.7 171.0 %all-gather.13.cloned.1.call-start = ((), (), s32[]{:S(2)}) async-start(), calls=%async_computation.9 | async-start | bytes 3981312 | tf_op jit(solution)/shard_map/all_gather | solution.py:199
  9.4 556.7 %all-gather.11.cloned.1.call-start = ((), (), s32[]{:S(2)}) async-start(), calls=%async_computation.8 | async-start | bytes 3981312 | tf_op jit(solution)/shard_map/all_gather | solution.py:200
  10.0 562.9 %all-gather.19.cloned.1.call-start = ((), (), s32[]{:S(2)}) async-start(), calls=%async_computation.12 | async-start | bytes 3981312 | tf_op jit(solution)/shard_map/all_gather | solution.py:201
  10.6 656.4 %all-reduce.8.cloned.1.call-start = ((), (), s32[]{:S(2)}) async-start(), calls=%async_computation.13 | async-start | bytes 8388608 | tf_op jit(solution)/shard_map/psum | solution.py:254
  188.2 52.4 %collective-permute-start = (f32[2,2,256,432]{2,3,1,0:T(8,128)}, f32[2,2,256,432]{2,3,1,0:T(8,128)S(1)}, u32[]{:S(2)}, u32[]{:S(2)}) collective-permute-start(f32[2,2,256,432]{2,3,1,0:T(8,128)} %multiply_add_fusion.5), channel_id=1, source_target_pairs={{0,4},{4,8},{8,12},{12,16},{16,20},{20,24},{24,28},{1,5},{5,9},{9,... | collective-permute-start | bytes 5308424 | tf_op jit(solution)/shard_map/while/body/eval_jaxpr/ppermute | solution.py:20
  242.2 65.5 %collective-permute-start = (f32[2,2,256,432]{2,3,1,0:T(8,128)}, f32[2,2,256,432]{2,3,1,0:T(8,128)S(1)}, u32[]{:S(2)}, u32[]{:S(2)}) collective-permute-start(f32[2,2,256,432]{2,3,1,0:T(8,128)} %multiply_add_fusion.5), channel_id=1, source_target_pairs={{0,4},{4,8},{8,12},{12,16},{16,20},{20,24},{24,28},{1,5},{5,9},{9,... | collective-permute-start | bytes 5308424 | tf_op jit(solution)/shard_map/while/body/eval_jaxpr/ppermute | solution.py:20
  309.3 68.5 %collective-permute-start = (f32[2,2,256,432]{2,3,1,0:T(8,128)}, f32[2,2,256,432]{2,3,1,0:T(8,128)S(1)}, u32[]{:S(2)}, u32[]{:S(2)}) collective-permute-start(f32[2,2,256,432]{2,3,1,0:T(8,128)} %multiply_add_fusion.5), channel_id=1, source_target_pairs={{0,4},{4,8},{8,12},{12,16},{16,20},{20,24},{24,28},{1,5},{5,9},{9,... | collective-permute-start | bytes 5308424 | tf_op jit(solution)/shard_map/while/body/eval_jaxpr/ppermute | solution.py:20
  379.3 51.4 %collective-permute-start = (f32[2,2,256,432]{2,3,1,0:T(8,128)}, f32[2,2,256,432]{2,3,1,0:T(8,128)S(1)}, u32[]{:S(2)}, u32[]{:S(2)}) collective-permute-start(f32[2,2,256,432]{2,3,1,0:T(8,128)} %multiply_add_fusion.5), channel_id=1, source_target_pairs={{0,4},{4,8},{8,12},{12,16},{16,20},{20,24},{24,28},{1,5},{5,9},{9,... | collective-permute-start | bytes 5308424 | tf_op jit(solution)/shard_map/while/body/eval_jaxpr/ppermute | solution.py:20
  432.3 42.1 %collective-permute-start = (f32[2,2,256,432]{2,3,1,0:T(8,128)}, f32[2,2,256,432]{2,3,1,0:T(8,128)S(1)}, u32[]{:S(2)}, u32[]{:S(2)}) collective-permute-start(f32[2,2,256,432]{2,3,1,0:T(8,128)} %multiply_add_fusion.5), channel_id=1, source_target_pairs={{0,4},{4,8},{8,12},{12,16},{16,20},{20,24},{24,28},{1,5},{5,9},{9,... | collective-permute-start | bytes 5308424 | tf_op jit(solution)/shard_map/while/body/eval_jaxpr/ppermute | solution.py:20
  476.0 41.2 %collective-permute-start = (f32[2,2,256,432]{2,3,1,0:T(8,128)}, f32[2,2,256,432]{2,3,1,0:T(8,128)S(1)}, u32[]{:S(2)}, u32[]{:S(2)}) collective-permute-start(f32[2,2,256,432]{2,3,1,0:T(8,128)} %multiply_add_fusion.5), channel_id=1, source_target_pairs={{0,4},{4,8},{8,12},{12,16},{16,20},{20,24},{24,28},{1,5},{5,9},{9,... | collective-permute-start | bytes 5308424 | tf_op jit(solution)/shard_map/while/body/eval_jaxpr/ppermute | solution.py:20
  518.8 40.4 %collective-permute-start = (f32[2,2,256,432]{2,3,1,0:T(8,128)}, f32[2,2,256,432]{2,3,1,0:T(8,128)S(1)}, u32[]{:S(2)}, u32[]{:S(2)}) collective-permute-start(f32[2,2,256,432]{2,3,1,0:T(8,128)} %multiply_add_fusion.5), channel_id=1, source_target_pairs={{0,4},{4,8},{8,12},{12,16},{16,20},{20,24},{24,28},{1,5},{5,9},{9,... | collective-permute-start | bytes 5308424 | tf_op jit(solution)/shard_map/while/body/eval_jaxpr/ppermute | solution.py:20
  579.6 156.7 %all-gather.21.cloned.1.call-start = ((), (), s32[]{:S(2)}) async-start(), calls=%async_computation.14 | async-start | bytes 3981312 | tf_op jit(solution)/shard_map/all_gather | solution.py:202
  580.4 223.4 %all-gather.23.cloned.1.call-start = ((), (), s32[]{:S(2)}) async-start(), calls=%async_computation.15 | async-start | bytes 3981312 | tf_op jit(solution)/shard_map/all_gather | solution.py:203
  581.1 290.1 %all-gather.25.cloned.1.call-start = ((), (), s32[]{:S(2)}) async-start(), calls=%async_computation.16 | async-start | bytes 3981312 | tf_op jit(solution)/shard_map/all_gather | solution.py:204
  581.9 387.7 %all-reduce.10.cloned.1.call-start = ((), (), s32[]{:S(2)}) async-start(), calls=%async_computation.17 | async-start | bytes 8388608 | tf_op jit(solution)/shard_map/psum | solution.py:296
  885.8 588.1 %all-reduce.12.cloned.1.call-start = ((), (), s32[]{:S(2)}) async-start(), calls=%async_computation.26 | async-start | bytes 16777216 | tf_op jit(solution)/shard_map/psum | solution.py:262
  1002.6 42.1 %collective-permute-start.1 = (f32[2,2,256,432]{2,3,1,0:T(8,128)}, f32[2,2,256,432]{2,3,1,0:T(8,128)S(1)}, u32[]{:S(2)}, u32[]{:S(2)}) collective-permute-start(f32[2,2,256,432]{2,3,1,0:T(8,128)} %multiply_add_fusion.6), channel_id=1, source_target_pairs={{4,0},{8,4},{12,8},{16,12},{20,16},{24,20},{28,24},{5,1},{9,5},{13... | collective-permute-start | bytes 5308424 | tf_op jit(solution)/shard_map/while/body/eval_jaxpr/ppermute | solution.py:20
  1046.2 41.9 %collective-permute-start.1 = (f32[2,2,256,432]{2,3,1,0:T(8,128)}, f32[2,2,256,432]{2,3,1,0:T(8,128)S(1)}, u32[]{:S(2)}, u32[]{:S(2)}) collective-permute-start(f32[2,2,256,432]{2,3,1,0:T(8,128)} %multiply_add_fusion.6), channel_id=1, source_target_pairs={{4,0},{8,4},{12,8},{16,12},{20,16},{24,20},{28,24},{5,1},{9,5},{13... | collective-permute-start | bytes 5308424 | tf_op jit(solution)/shard_map/while/body/eval_jaxpr/ppermute | solution.py:20
  1089.7 41.3 %collective-permute-start.1 = (f32[2,2,256,432]{2,3,1,0:T(8,128)}, f32[2,2,256,432]{2,3,1,0:T(8,128)S(1)}, u32[]{:S(2)}, u32[]{:S(2)}) collective-permute-start(f32[2,2,256,432]{2,3,1,0:T(8,128)} %multiply_add_fusion.6), channel_id=1, source_target_pairs={{4,0},{8,4},{12,8},{16,12},{20,16},{24,20},{28,24},{5,1},{9,5},{13... | collective-permute-start | bytes 5308424 | tf_op jit(solution)/shard_map/while/body/eval_jaxpr/ppermute | solution.py:20
  1132.5 40.5 %collective-permute-start.1 = (f32[2,2,256,432]{2,3,1,0:T(8,128)}, f32[2,2,256,432]{2,3,1,0:T(8,128)S(1)}, u32[]{:S(2)}, u32[]{:S(2)}) collective-permute-start(f32[2,2,256,432]{2,3,1,0:T(8,128)} %multiply_add_fusion.6), channel_id=1, source_target_pairs={{4,0},{8,4},{12,8},{16,12},{20,16},{24,20},{28,24},{5,1},{9,5},{13... | collective-permute-start | bytes 5308424 | tf_op jit(solution)/shard_map/while/body/eval_jaxpr/ppermute | solution.py:20
  1174.6 39.6 %collective-permute-start.1 = (f32[2,2,256,432]{2,3,1,0:T(8,128)}, f32[2,2,256,432]{2,3,1,0:T(8,128)S(1)}, u32[]{:S(2)}, u32[]{:S(2)}) collective-permute-start(f32[2,2,256,432]{2,3,1,0:T(8,128)} %multiply_add_fusion.6), channel_id=1, source_target_pairs={{4,0},{8,4},{12,8},{16,12},{20,16},{24,20},{28,24},{5,1},{9,5},{13... | collective-permute-start | bytes 5308424 | tf_op jit(solution)/shard_map/while/body/eval_jaxpr/ppermute | solution.py:20
  1215.7 38.7 %collective-permute-start.1 = (f32[2,2,256,432]{2,3,1,0:T(8,128)}, f32[2,2,256,432]{2,3,1,0:T(8,128)S(1)}, u32[]{:S(2)}, u32[]{:S(2)}) collective-permute-start(f32[2,2,256,432]{2,3,1,0:T(8,128)} %multiply_add_fusion.6), channel_id=1, source_target_pairs={{4,0},{8,4},{12,8},{16,12},{20,16},{24,20},{28,24},{5,1},{9,5},{13... | collective-permute-start | bytes 5308424 | tf_op jit(solution)/shard_map/while/body/eval_jaxpr/ppermute | solution.py:20
  1318.3 248.4 %reduce-scatter.11.cloned.1.call-start = ((), (), s32[]{:S(2)}) async-start(), calls=%async_computation.19 | async-start | bytes 4718592 | tf_op jit(solution)/shard_map/reduce_scatter | solution.py:357
  1323.3 335.6 %reduce-scatter.9.cloned.1.call-start = ((), (), s32[]{:S(2)}) async-start(), calls=%async_computation.18 | async-start | bytes 4718592 | tf_op jit(solution)/shard_map/reduce_scatter | solution.py:356
  1326.7 465.5 %reduce-scatter.19.cloned.1.call-start = ((), (), s32[]{:S(2)}) async-start(), calls=%async_computation.23 | async-start | bytes 7962624 | tf_op jit(solution)/shard_map/reduce_scatter | solution.py:361
  1334.4 590.7 %reduce-scatter.21.cloned.1.call-start = ((), (), s32[]{:S(2)}) async-start(), calls=%async_computation.24 | async-start | bytes 7962624 | tf_op jit(solution)/shard_map/reduce_scatter | solution.py:362
  1342.1 715.9 %reduce-scatter.23.cloned.1.call-start = ((), (), s32[]{:S(2)}) async-start(), calls=%async_computation.25 | async-start | bytes 7962624 | tf_op jit(solution)/shard_map/reduce_scatter | solution.py:363
  1349.8 841.0 %reduce-scatter.17.cloned.1.call-start = ((), (), s32[]{:S(2)}) async-start(), calls=%async_computation.22 | async-start | bytes 7962624 | tf_op jit(solution)/shard_map/reduce_scatter | solution.py:360
  1358.1 965.6 %reduce-scatter.13.cloned.1.call-start = ((), (), s32[]{:S(2)}) async-start(), calls=%async_computation.20 | async-start | bytes 7962624 | tf_op jit(solution)/shard_map/reduce_scatter | solution.py:358
  1364.2 1092.5 %reduce-scatter.15.cloned.1.call-start = ((), (), s32[]{:S(2)}) async-start(), calls=%async_computation.21 | async-start | bytes 7962624 | tf_op jit(solution)/shard_map/reduce_scatter | solution.py:359
  (69 other events, 1905.7 us)
Sparse Core Ops, SparseCore 0:
  10.1 51.9 all-gather.16
  64.2 47.6 all-gather.14
  113.9 65.6 all-gather.12
  181.6 92.4 all-gather.10
  276.0 88.9 all-gather.18
  579.7 87.2 all-reduce.7
  669.1 67.2 all-gather.20
  738.4 65.3 all-gather.22
  805.8 65.3 all-gather.24
  885.9 83.6 all-reduce.9
  1318.5 155.3 all-reduce.11
  1477.9 88.8 reduce-scatter.10
  1571.0 87.9 reduce-scatter.8
  1663.1 129.1 reduce-scatter.18
  1796.4 128.6 reduce-scatter.20
  1929.2 128.6 reduce-scatter.22
  2062.1 128.6 reduce-scatter.16
  2195.0 128.6 reduce-scatter.12
  2327.9 128.6 reduce-scatter.14
where the time goes:
time: 2470 us; the launch traced here: 2460 us
  waiting for transfers between devices  2050 us (83%)
  matrix products  132 us (5%)
  starting transfers between devices  84.9 us (3%)
  blocking collectives  80.8 us (3%)
  other arithmetic  62.5 us (3%)
  local copies, waits for them, and re-layouts  37.6 us (2%)
    ppermute x14, waiting for transfers between devices, passed_along(): return lax.ppermute(block, axis, route)  560 us
    reduce_scatter x1, waiting for transfers between devices, on_device(): lax.psum_scatter(glu_grad, 'seq', scatter_dimension=0, tiled=True)  133 us
    reduce_scatter x1, waiting for transfers between devices, on_device(): lax.psum_scatter(gate_grad, 'seq', scatter_dimension=0, tiled=True)  133 us
    reduce_scatter x1, waiting for transfers between devices, on_device(): lax.psum_scatter(down_grad, 'seq', scatter_dimension=1, tiled=True)  133 us
    reduce_scatter x1, waiting for transfers between devices, on_device(): lax.psum_scatter(value_grad, 'seq', scatter_dimension=0, tiled=True)  133 us
    reduce_scatter x1, waiting for transfers between devices, on_device(): lax.psum_scatter(out_grad, 'seq', scatter_dimension=1, tiled=True)  133 us
    reduce_scatter x1, waiting for transfers between devices, on_device(): lax.psum_scatter(up_grad, 'seq', scatter_dimension=0, tiled=True)  133 us
    psum x1, waiting for transfers between devices, on_device(): lax.psum(jnp.dot(hidden, full_down, preferred_element_type=jnp.float32),...  101 us
  transfers between devices with their start and end apart: 33, of which 31 were waited for; matrix products, arithmetic and copies ran while one was open for 5% of the time, Pallas kernels for 0%

commit v1 on v0

v1 whole, which is shorter than its diff:
```python
import functools
import math

import jax
import jax.numpy as jnp
from jax import lax
from jax.experimental import pallas as pl
from jax.experimental.pallas import tpu as pltpu
from jax.sharding import PartitionSpec as P

KEY = 256
VAL = 432
EPS_LAYER = 1e-05
EPS_GROUP = 1e-06
BF = jnp.bfloat16
F32 = jnp.float32
MESH = pl.DeviceIdType.MESH
CHUNKS = 2
RS_MSGS = 10
AG_MSGS = 9


def normalize(values, epsilon):
    average = jnp.mean(values, axis=-1, keepdims=True)
    centred = values - average
    inv_std = lax.rsqrt(jnp.mean(centred * centred, axis=-1, keepdims=True) + epsilon)
    return centred * inv_std, inv_std


def normalize_back(upstream, normed, inv_std):
    return inv_std * (
        upstream
        - jnp.mean(upstream, axis=-1, keepdims=True)
        - normed * jnp.mean(upstream * normed, axis=-1, keepdims=True)
    )


def swish_parts(values):
    sigmoid = jax.nn.sigmoid(values)
    return values * sigmoid, sigmoid * (1.0 + values * (1.0 - sigmoid))


class Spot:
    def __init__(self):
        seq, tp = lax.axis_index("seq"), lax.axis_index("tp")
        self.x = lax.rem(seq, 2)
        self.y = tp // 2
        self.c = lax.rem(tp, 2)
        self.to_x = (seq + 1 - 2 * self.x, tp)
        self.to_y = (seq, tp + 2 - 4 * self.y)
        self.to_c = (seq, tp + 1 - 2 * self.c)

    def meet(self):
        barrier = pltpu.get_barrier_semaphore()
        for partner in (self.to_x, self.to_y, self.to_c):
            pl.semaphore_signal(barrier, inc=1, device_id=partner, device_id_type=MESH)
        pl.semaphore_wait(barrier, 3)


class Post:
    def __init__(self, send_sem, recv_sem, base):
        self.send_sem, self.recv_sem, self.base = send_sem, recv_sem, base
        self.sent = []

    def send(self, index, src, dst, partner):
        copy = pltpu.make_async_remote_copy(
            src_ref=src,
            dst_ref=dst,
            send_sem=self.send_sem.at[self.base + index],
            recv_sem=self.recv_sem.at[self.base + index],
            device_id=partner,
            device_id_type=MESH,
        )
        copy.start()
        self.sent.append(copy)
        return copy

    def finish(self):
        for copy in self.sent:
            copy.wait_send()


def sum_steps(spot, post, part, held, rows, width):
    from_core, staged, from_x, from_y = held
    half = width // 2
    low, high = pl.ds(0, half), pl.ds(half, half)
    x, y, c = spot.x, spot.y, spot.c
    blocks = ((1 - y, 1 - x), (y, 1 - x), (1 - y, x), (y, x))
    core = []
    for i, (yb, xb) in enumerate(blocks):
        core.append(
            post.send(i, part.at[yb, xb, 1 - c, rows], from_core.at[i, rows], spot.to_c)
        )
    yield

    def own(i, cols):
        yb, xb = blocks[i]
        return part[yb, xb, c, rows, cols].astype(F32) + from_core[i, rows, cols].astype(F32)

    core[0].wait_recv()
    staged[0, rows, :] = own(0, pl.ds(0, width)).astype(BF)
    a1 = post.send(4, staged.at[0, rows, low], from_x.at[0, rows], spot.to_x)
    b1 = post.send(5, staged.at[0, rows, high], from_y.at[0, rows], spot.to_y)
    core[1].wait_recv()
    staged[1, rows, low] = own(1, low).astype(BF)
    a2 = post.send(6, staged.at[1, rows, low], from_x.at[1, rows], spot.to_x)
    core[2].wait_recv()
    staged[2, rows, high] = own(2, high).astype(BF)
    b2 = post.send(7, staged.at[2, rows, high], from_y.at[1, rows], spot.to_y)
    yield
    b1.wait_recv()
    staged[1, rows, high] = (own(1, high) + from_y[0, rows, :].astype(F32)).astype(BF)
    b3 = post.send(8, staged.at[1, rows, high], from_x.at[2, rows], spot.to_x)
    a1.wait_recv()
    staged[2, rows, low] = (own(2, low) + from_x[0, rows, :].astype(F32)).astype(BF)
    a3 = post.send(9, staged.at[2, rows, low], from_y.at[2, rows], spot.to_y)
    core[3].wait_recv()
    yield
    a2.wait_recv()
    b2.wait_recv()
    b3.wait_recv()
    a3.wait_recv()
    left = own(3, low) + from_x[1, rows, :].astype(F32) + from_y[2, rows, :].astype(F32)
    right = own(3, high) + from_y[1, rows, :].astype(F32) + from_x[2, rows, :].astype(F32)
    return jnp.concatenate([left, right], axis=-1)


def spread_steps(spot, post, full, rows, width):
    half = width // 2
    low, high = pl.ds(0, half), pl.ds(half, half)
    x, y, c = spot.x, spot.y, spot.c
    mine = full.at[y, x, c, rows]
    by_x = post.send(0, mine, mine, spot.to_x)
    by_y = post.send(1, mine, mine, spot.to_y)
    waits = [post.send(2, mine, mine, spot.to_c)]
    yield
    by_x.wait_recv()
    block = full.at[y, 1 - x, c, rows, low]
    diag_low = post.send(3, block, block, spot.to_y)
    block = full.at[y, 1 - x, c, rows]
    waits.append(post.send(4, block, block, spot.to_c))
    by_y.wait_recv()
    block = full.at[1 - y, x, c, rows, high]
    diag_high = post.send(5, block, block, spot.to_x)
    block = full.at[1 - y, x, c, rows]
    waits.append(post.send(6, block, block, spot.to_c))
    yield
    diag_low.wait_recv()
    block = full.at[1 - y, 1 - x, c, rows, low]
    waits.append(post.send(7, block, block, spot.to_c))
    diag_high.wait_recv()
    block = full.at[1 - y, 1 - x, c, rows, high]
    waits.append(post.send(8, block, block, spot.to_c))
    yield
    for copy in waits:
        copy.wait_recv()


def spread_four_steps(spot, post, full, rows):
    y, c = spot.y, spot.c
    mine = full.at[y, c, rows]
    by_y = post.send(0, mine, mine, spot.to_y)
    waits = [post.send(1, mine, mine, spot.to_c)]
    yield
    by_y.wait_recv()
    block = full.at[1 - y, c, rows]
    waits.append(post.send(2, block, block, spot.to_c))
    yield
    for copy in waits:
        copy.wait_recv()


def run_all(tasks):
    tasks = list(tasks)
    while tasks:
        alive = []
        for task in tasks:
            try:
                next(task)
                alive.append(task)
            except StopIteration:
                pass
        tasks = alive


def row_chunks(count):
    size = count // CHUNKS
    return [pl.ds(i * size, size) for i in range(CHUNKS)]


def whole_specs(count):
    return [pl.BlockSpec(memory_space=pltpu.VMEM)] * count


def rs_scratch(rows, width):
    return [
        pltpu.VMEM((4, rows, width), BF),
        pltpu.VMEM((3, rows, width), BF),
        pltpu.VMEM((3, rows, width // 2), BF),
        pltpu.VMEM((3, rows, width // 2), BF),
    ]


def params(collective_id):
    return pltpu.CompilerParams(collective_id=collective_id, has_side_effects=True)


def entry_kernel(
    rows_ref, gain_ref, normed_ref, inv_ref, gains_ref, full, held, send_sem, recv_sem, far_send, far_recv
):
    spot = Spot()
    count, width = rows_ref.shape
    ranks = held.shape[0]
    me = lax.axis_index("seq")
    tp = lax.axis_index("tp")
    barrier = pltpu.get_barrier_semaphore()
    partners = [spot.to_y, spot.to_c]
    partners += [(lax.rem(me + k, ranks), tp) for k in range(1, ranks)]
    for partner in partners:
        pl.semaphore_signal(barrier, inc=1, device_id=partner, device_id_type=MESH)
    pl.semaphore_wait(barrier, len(partners))
    far = []
    for k in range(1, ranks):
        copy = pltpu.make_async_remote_copy(
            src_ref=gain_ref,
            dst_ref=held.at[k],
            send_sem=far_send.at[k],
            recv_sem=far_recv.at[k],
            device_id=(lax.rem(me + k, ranks), tp),
            device_id_type=MESH,
        )
        copy.start()
        far.append(copy)
    held[0] = gain_ref[...]
    for rows in row_chunks(count):
        normed, inv_std = normalize(rows_ref[rows, :].astype(F32), EPS_LAYER)
        normed_ref[rows, :] = normed
        inv_ref[rows, :] = inv_std
    for copy in far:
        copy.wait_recv()
    gains_ref[...] = jnp.concatenate(
        [held[lax.rem(me - r + ranks, ranks)] for r in range(ranks)], axis=-1
    )
    gain = gains_ref[0:1, :]
    posts, tasks = [], []
    for i, rows in enumerate(row_chunks(count)):
        full[spot.y, spot.x, spot.c, rows, :] = (normed_ref[rows, :] * gain).astype(BF)
        post = Post(send_sem, recv_sem, i * AG_MSGS)
        task = spread_steps(spot, post, full, rows, width)
        next(task)
        posts.append(post)
        tasks.append(task)
    run_all(tasks)
    for post in posts:
        post.finish()
    for copy in far:
        copy.wait_send()


def entry(rows, gains, ranks):
    count, width = rows.shape
    return pl.pallas_call(
        entry_kernel,
        name="entry",
        out_shape=(
            jax.ShapeDtypeStruct((count, width), F32),
            jax.ShapeDtypeStruct((count, 1), F32),
            jax.ShapeDtypeStruct((8, width), F32),
            jax.ShapeDtypeStruct((2, 2, 2, count, width), BF),
        ),
        in_specs=whole_specs(2),
        out_specs=tuple(whole_specs(4)),
        scratch_shapes=[
            pltpu.VMEM((ranks, 8, width // ranks), F32),
            pltpu.SemaphoreType.DMA((CHUNKS * AG_MSGS,)),
            pltpu.SemaphoreType.DMA((CHUNKS * AG_MSGS,)),
            pltpu.SemaphoreType.DMA((ranks,)),
            pltpu.SemaphoreType.DMA((ranks,)),
        ],
        compiler_params=params(1),
    )(rows, gains)


def middle_kernel(
    part, rows_ref, gains_ref, mid_ref, normed_ref, inv_ref, full, h0, h1, h2, h3, send_sem, recv_sem
):
    spot = Spot()
    count, width = rows_ref.shape
    spot.meet()
    posts = []

    def chain(i, rows):
        post = Post(send_sem, recv_sem, i * (RS_MSGS + AG_MSGS))
        posts.append(post)
        total = yield from sum_steps(spot, post, part, (h0, h1, h2, h3), rows, width)
        middle = rows_ref[rows, :].astype(F32) + total
        normed, inv_std = normalize(middle, EPS_LAYER)
        mid_ref[rows, :] = middle
        normed_ref[rows, :] = normed
        inv_ref[rows, :] = inv_std
        full[spot.y, spot.x, spot.c, rows, :] = (normed * gains_ref[1:2, :]).astype(BF)
        post = Post(send_sem, recv_sem, i * (RS_MSGS + AG_MSGS) + RS_MSGS)
        posts.append(post)
        yield from spread_steps(spot, post, full, rows, width)

    run_all(chain(i, rows) for i, rows in enumerate(row_chunks(count)))
    for post in posts:
        post.finish()


def middle_stage(part, rows, gains):
    count, width = rows.shape
    sems = CHUNKS * (RS_MSGS + AG_MSGS)
    return pl.pallas_call(
        middle_kernel,
        name="middle",
        out_shape=(
            jax.ShapeDtypeStruct((count, width), F32),
            jax.ShapeDtypeStruct((count, width), F32),
            jax.ShapeDtypeStruct((count, 1), F32),
            jax.ShapeDtypeStruct((2, 2, 2, count, width), BF),
        ),
        in_specs=whole_specs(3),
        out_specs=tuple(whole_specs(4)),
        scratch_shapes=rs_scratch(count, width)
        + [pltpu.SemaphoreType.DMA((sems,)), pltpu.SemaphoreType.DMA((sems,))],
        compiler_params=params(2),
    )(part, rows, gains)


def turn_kernel(
    part, cot_ref, gains_ref, normed_ref, inv_ref, grad_ref, full, h0, h1, h2, h3, send_sem, recv_sem
):
    spot = Spot()
    count, width = cot_ref.shape
    spot.meet()
    posts = []

    def chain(i, rows):
        post = Post(send_sem, recv_sem, i * (RS_MSGS + AG_MSGS))
        posts.append(post)
        total = yield from sum_steps(spot, post, part, (h0, h1, h2, h3), rows, width)
        grad = cot_ref[rows, :].astype(F32) + normalize_back(
            total * gains_ref[1:2, :], normed_ref[rows, :], inv_ref[rows, :]
        )
        grad_ref[rows, :] = grad
        full[spot.y, spot.x, spot.c, rows, :] = grad.astype(BF)
        post = Post(send_sem, recv_sem, i * (RS_MSGS + AG_MSGS) + RS_MSGS)
        posts.append(post)
        yield from spread_steps(spot, post, full, rows, width)

    run_all(chain(i, rows) for i, rows in enumerate(row_chunks(count)))
    for post in posts:
        post.finish()


def turn_stage(part, cot, gains, normed, inv_std):
    count, width = cot.shape
    sems = CHUNKS * (RS_MSGS + AG_MSGS)
    return pl.pallas_call(
        turn_kernel,
        name="turn",
        out_shape=(
            jax.ShapeDtypeStruct((count, width), F32),
            jax.ShapeDtypeStruct((2, 2, 2, count, width), BF),
        ),
        in_specs=whole_specs(5),
        out_specs=tuple(whole_specs(2)),
        scratch_shapes=rs_scratch(count, width)
        + [pltpu.SemaphoreType.DMA((sems,)), pltpu.SemaphoreType.DMA((sems,))],
        compiler_params=params(3),
    )(part, cot, gains, normed, inv_std)


LAST_MSGS = 2 * (RS_MSGS + 3)


def last_kernel(
    part_in,
    part_out,
    gains_ref,
    normed_ref,
    inv_ref,
    grad_ref,
    mid_ref,
    input_full,
    out_full,
    g0,
    g1,
    g2,
    g3,
    h0,
    h1,
    h2,
    h3,
    send_sem,
    recv_sem,
):
    spot = Spot()
    count, width = mid_ref.shape
    spot.meet()
    posts = []

    def chain_in(i, rows):
        post = Post(send_sem, recv_sem, i * LAST_MSGS)
        posts.append(post)
        total = yield from sum_steps(spot, post, part_in, (g0, g1, g2, g3), rows, width)
        input_full[spot.y, spot.c, rows, :] = grad_ref[rows, :] + normalize_back(
            total * gains_ref[0:1, :], normed_ref[rows, :], inv_ref[rows, :]
        )
        post = Post(send_sem, recv_sem, i * LAST_MSGS + RS_MSGS)
        posts.append(post)
        yield from spread_four_steps(spot, post, input_full, rows)

    def chain_out(i, rows):
        base = i * LAST_MSGS + RS_MSGS + 3
        post = Post(send_sem, recv_sem, base)
        posts.append(post)
        total = yield from sum_steps(spot, post, part_out, (h0, h1, h2, h3), rows, width)
        out_full[spot.y, spot.c, rows, :] = (mid_ref[rows, :] + total).astype(BF)
        post = Post(send_sem, recv_sem, base + RS_MSGS)
        posts.append(post)
        yield from spread_four_steps(spot, post, out_full, rows)

    tasks = [chain_in(i, rows) for i, rows in enumerate(row_chunks(count))]
    tasks += [chain_out(i, rows) for i, rows in enumerate(row_chunks(count))]
    run_all(tasks)
    for post in posts:
        post.finish()


def last_stage(part_in, part_out, gains, normed, inv_std, grad, middle):
    count, width = middle.shape
    sems = CHUNKS * LAST_MSGS
    return pl.pallas_call(
        last_kernel,
        name="last",
        out_shape=(
            jax.ShapeDtypeStruct((2, 2, count, width), F32),
            jax.ShapeDtypeStruct((2, 2, count, width), BF),
        ),
        in_specs=whole_specs(7),
        out_specs=tuple(whole_specs(2)),
        scratch_shapes=rs_scratch(count, width)
        + rs_scratch(count, width)
        + [pltpu.SemaphoreType.DMA((sems,)), pltpu.SemaphoreType.DMA((sems,))],
        compiler_params=params(4),
    )(part_in, part_out, gains, normed, inv_std, grad, middle)


def rotary_tables(positions, width):
    half_width = width // 2
    fraction = jnp.arange(half_width, dtype=F32) / max(half_width - 1, 1)
    frequency = jnp.power(10000.0, -fraction)
    angles = positions[:, None] * frequency[None, :]
    cosine = jnp.concatenate([jnp.cos(angles), jnp.cos(angles)], axis=-1)
    sine = jnp.concatenate([jnp.sin(angles), jnp.sin(angles)], axis=-1)
    return cosine, sine


def rotate(values, cosine, sine):
    half_width = values.shape[-1] // 2
    turned = jnp.concatenate([-values[..., half_width:], values[..., :half_width]], axis=-1)
    return values * cosine + turned * sine


def rotate_back(upstream, cosine, sine):
    half_width = upstream.shape[-1] // 2
    scaled = upstream * sine
    turned = jnp.concatenate([scaled[..., half_width:], -scaled[..., :half_width]], axis=-1)
    return upstream * cosine + turned


def product(spec, left, right):
    return jnp.einsum(spec, left, right, preferred_element_type=F32)


def shifted(block, distance):
    devices = range(lax.axis_size("seq"))
    route = [(i - distance, i) for i in devices if i - distance in devices]
    return lax.ppermute(block, "seq", route)


def carried(summary, decay, direction):
    planes = lax.axis_size("seq") // 2
    if planes <= 4:
        total = 0.0
        packed = summary.astype(BF)
        for k in range(1, planes):
            total = total + decay ** (k - 1) * shifted(packed, 2 * k * direction).astype(F32)
        return total
    state = shifted(summary.astype(BF), 2 * direction).astype(F32)
    reach = 1
    while reach < planes:
        state = state + decay**reach * shifted(state.astype(BF), 2 * reach * direction).astype(F32)
        reach *= 2
    return state


def on_device(
    inputs,
    cotangent,
    attn_gain,
    w_query,
    w_key,
    w_value,
    w_gate,
    w_out,
    ffn_gain,
    w_glu,
    w_up,
    w_down,
    decay_rate,
):
    seqs, tok_rows, width = inputs.shape
    seq_size = lax.axis_size("seq")
    planes = seq_size // 2
    quarter = tok_rows // 2
    span = 2 * tok_rows
    tokens = seqs * span
    seq_at, tp_at = lax.axis_index("seq"), lax.axis_index("tp")
    x_at, plane = lax.rem(seq_at, 2), seq_at // 2
    y_at, c_at = tp_at // 2, lax.rem(tp_at, 2)
    pairs = [(i, i + 1 - 2 * (i % 2)) for i in range(seq_size)]
    rings = [[2 * z + x for z in range(planes)] for x in range(2)]

    def own_rows(array):
        rows = lax.dynamic_slice(array, (y_at, c_at * quarter, 0), (1, quarter, width))
        return rows.reshape(quarter, width)

    def halves(array):
        half = array.shape[1] // 2
        low, high = array[:, :half], array[:, half:]
        return jnp.where(x_at == 0, low, high), jnp.where(x_at == 0, high, low)

    def gathered(parts):
        mine = [halves(p) for p in parts]
        kept = jnp.concatenate([m[0] for m in mine], axis=1)
        other = lax.ppermute(jnp.concatenate([m[1] for m in mine], axis=1), "seq", pairs)
        both = jnp.concatenate(
            [jnp.where(x_at == 0, kept, other), jnp.where(x_at == 0, other, kept)], axis=0
        )
        return lax.all_gather(both, "seq", axis_index_groups=rings, axis=0, tiled=True)

    full_qk = gathered([w_query, w_key])
    full_vg = gathered([w_value, w_gate])
    full_out = gathered([w_out.T])
    full_gu = gathered([w_glu, w_up])
    full_down = gathered([w_down.T])
    full_value, full_gate = full_vg[:, :VAL], full_vg[:, VAL:]
    units = full_gu.shape[1] // 2
    full_glu, full_up = full_gu[:, :units], full_gu[:, units:]

    my_inputs = own_rows(inputs)
    my_cot = own_rows(cotangent)
    own_gains = jnp.stack([attn_gain, ffn_gain] + [attn_gain] * 6).astype(F32)
    normed_one, inv_one, gains, spread_one = entry(my_inputs, own_gains, seq_size)
    attn_in = spread_one.reshape(tokens, width)

    qk_lin = product("td,dn->tn", attn_in, full_qk)
    value_rows = product("td,dn->tn", attn_in, full_value).astype(BF).reshape(seqs, span, VAL)
    gate_lin = product("td,dn->tn", attn_in, full_gate)

    positions = (plane * span).astype(F32) + jnp.arange(span, dtype=F32)
    cosine, sine = rotary_tables(positions, KEY)
    key_scale = 1.0 / math.sqrt(KEY)
    rate = jnp.where(x_at == 0, decay_rate[0], decay_rate[1])
    query_rot = rotate(qk_lin[:, :KEY].reshape(seqs, span, KEY), cosine, sine).astype(BF)
    key_rot = (rotate(qk_lin[:, KEY:].reshape(seqs, span, KEY), cosine, sine) * key_scale).astype(
        BF
    )
    offsets = jnp.arange(span, dtype=F32)
    distance = offsets[:, None] - offsets[None, :]
    mask = jnp.where(distance >= 0.0, jnp.exp(-rate * jnp.maximum(distance, 0.0)), 0.0)
    leading = jnp.exp(-rate * (offsets + 1.0))[:, None]
    trailing = jnp.exp(-rate * (span - 1.0 - offsets))[:, None]
    plane_decay = jnp.exp(-rate * span)

    summary = product("stk,stv->skv", (key_rot.astype(F32) * trailing).astype(BF), value_rows)
    state = carried(summary, plane_decay, 1).astype(BF)
    query_led = (query_rot.astype(F32) * leading).astype(BF)
    weights = (product("stk,smk->stm", query_rot, key_rot) * mask).astype(BF)
    retained = product("stm,smv->stv", weights, value_rows) + product(
        "stk,skv->stv", query_led, state
    )
    group_normed, group_inv = normalize(retained, EPS_GROUP)
    gate_act, gate_slope = swish_parts(gate_lin)
    group_flat = group_normed.reshape(tokens, VAL)
    mixed = (gate_act * group_flat).astype(BF)

    def as_blocks(rows):
        return rows.astype(BF).reshape(2, 2, 2, quarter, width)

    attn_part = as_blocks(product("tn,dn->td", mixed, full_out))
    middle, normed_two, inv_two, spread_two = middle_stage(attn_part, my_inputs, gains)
    ffn_in = spread_two.reshape(tokens, width)

    glu_lin = product("td,dn->tn", ffn_in, full_glu)
    up_lin = product("td,dn->tn", ffn_in, full_up)
    glu_act, glu_slope = swish_parts(glu_lin)
    hidden = (glu_act * up_lin).astype(BF)
    ffn_part = as_blocks(product("tn,dn->td", hidden, full_down))

    tp_flip = [(i, i + 1 - 2 * (i % 2)) for i in range(4)]
    tp_far = [(i, (i + 2) % 4) for i in range(4)]

    def in_order(mine, other, bit):
        return jnp.stack([jnp.where(bit == 0, mine, other), jnp.where(bit == 0, other, mine)])

    quarter_cot = lax.ppermute(my_cot, "seq", pairs)
    by_y = in_order(quarter_cot, lax.ppermute(quarter_cot, "tp", tp_far), y_at)
    by_c = in_order(by_y, lax.ppermute(by_y, "tp", tp_flip), c_at)
    other_cot = jnp.swapaxes(by_c, 0, 1).reshape(seqs, tok_rows, width)
    cot_rows = jnp.concatenate(
        [
            jnp.where(x_at == 0, cotangent, other_cot),
            jnp.where(x_at == 0, other_cot, cotangent),
        ],
        axis=1,
    ).reshape(tokens, width)

    def scattered(grad):
        return lax.psum_scatter(
            grad.astype(BF), "seq", axis_index_groups=rings, scatter_dimension=0, tiled=True
        )

    grad_hidden = product("td,dn->tn", cot_rows, full_down)
    grad_glu = (grad_hidden * up_lin * glu_slope).astype(BF)
    grad_up = (grad_hidden * glu_act).astype(BF)
    grad_gu = jnp.concatenate([grad_glu, grad_up], axis=1)
    ffn_grad_part = as_blocks(product("tn,dn->td", grad_gu, full_gu))
    down_sum = scattered(product("td,tn->dn", cot_rows, hidden))
    gu_sum = scattered(product("td,tn->dn", ffn_in, grad_gu))

    grad_middle, spread_three = turn_stage(ffn_grad_part, my_cot, gains, normed_two, inv_two)
    grad_rows = spread_three.reshape(tokens, width)
    out_sum = scattered(product("td,tn->dn", grad_rows, mixed))
    grad_mixed = product("td,dn->tn", grad_rows, full_out)
    grad_gate = (grad_mixed * group_flat * gate_slope).astype(BF)
    grad_group = (grad_mixed * gate_act).reshape(seqs, span, VAL)
    grad_retained_f32 = normalize_back(grad_group, group_normed, group_inv)
    grad_retained = grad_retained_f32.astype(BF)
    rest_retained = (grad_retained_f32 - lax.reduce_precision(grad_retained_f32, 8, 7)).astype(BF)

    own_grad = product("stk,stv->skv", query_led, grad_retained)
    state_grad = carried(own_grad, plane_decay, -1).astype(BF)
    pulls = product("stv,smv->stm", grad_retained, value_rows) + product(
        "stv,smv->stm", rest_retained, value_rows
    )
    grad_weights = (pulls * mask).astype(BF)
    grad_qrot = product("stm,smk->stk", grad_weights, key_rot) + leading * product(
        "stv,skv->stk", grad_retained, state
    )
    grad_krot = product("stm,stk->smk", grad_weights, query_rot) + trailing * product(
        "smv,skv->smk", value_rows, state_grad
    )
    grad_vrows = product("stm,stv->smv", weights, grad_retained) + trailing * product(
        "smk,skv->smv", key_rot, state_grad
    )
    grad_query = rotate_back(grad_qrot, cosine, sine).astype(BF).reshape(tokens, KEY)
    grad_key = (rotate_back(grad_krot, cosine, sine) * key_scale).astype(BF).reshape(tokens, KEY)
    grad_value = grad_vrows.astype(BF).reshape(tokens, VAL)
    grad_vqk = jnp.concatenate([grad_query, grad_key, grad_value], axis=1)

    gate_sum = scattered(product("td,tn->dn", attn_in, grad_gate))
    vqk_sum = scattered(product("td,tn->dn", attn_in, grad_vqk))
    attn_grad_part = as_blocks(
        product("tn,dn->td", grad_gate, full_gate)
        + product("tn,dn->td", grad_value, full_value)
        + product("tn,dn->td", grad_vqk[:, : 2 * KEY], full_qk)
    )
    input_full, out_full = last_stage(
        attn_grad_part, ffn_part, gains, normed_one, inv_one, grad_middle, middle
    )

    def returned(total):
        rows = total.shape[0] // 2
        low, high = total[:rows], total[rows:]
        kept = jnp.where(x_at == 0, low, high)
        other = lax.ppermute(jnp.where(x_at == 0, high, low), "seq", pairs)
        first = jnp.where(x_at == 0, kept, other).astype(F32)
        second = jnp.where(x_at == 0, other, kept).astype(F32)
        return first, second

    def joined(first, second):
        return jnp.concatenate([first, second], axis=1)

    first, second = returned(vqk_sum)
    query_grad = joined(first[:, :KEY], second[:, :KEY])
    key_grad = joined(first[:, KEY : 2 * KEY], second[:, KEY : 2 * KEY])
    value_grad = joined(first[:, 2 * KEY :], second[:, 2 * KEY :])
    gate_grad = joined(*returned(gate_sum))
    first, second = returned(gu_sum)
    glu_grad = joined(first[:, :units], second[:, :units])
    up_grad = joined(first[:, units:], second[:, units:])
    out_grad = joined(*returned(out_sum)).T
    down_grad = joined(*returned(down_sum)).T

    def gain_part(pairs_of):
        return sum(jnp.sum(w.astype(F32) * grad, axis=1) for w, grad in pairs_of)

    gain_grads = jnp.stack(
        [
            gain_part(
                [
                    (w_query, query_grad),
                    (w_key, key_grad),
                    (w_value, value_grad),
                    (w_gate, gate_grad),
                ]
            ),
            gain_part([(w_glu, glu_grad), (w_up, up_grad)]),
        ]
    )
    gain_grads = gain_grads + lax.ppermute(gain_grads, "tp", tp_flip)
    gain_grads = gain_grads + lax.ppermute(gain_grads, "tp", tp_far)
    gain_grads = gain_grads / own_gains[:2]

    return (
        out_full.reshape(seqs, tok_rows, width),
        input_full.reshape(seqs, tok_rows, width),
        gain_grads[0],
        query_grad,
        key_grad,
        value_grad,
        gate_grad,
        out_grad,
        gain_grads[1],
        glu_grad,
        up_grad,
        down_grad,
    )


def solution(mesh):
    return jax.shard_map(
        on_device,
        mesh=mesh,
        in_specs=(
            P(None, "seq", None),
            P(None, "seq", None),
            P("seq"),
            P("seq", "tp"),
            P("seq", "tp"),
            P("seq", "tp"),
            P("seq", "tp"),
            P("tp", "seq"),
            P("seq"),
            P("seq", "tp"),
            P("seq", "tp"),
            P("tp", "seq"),
            P("tp"),
        ),
        out_specs=(
            P(None, "seq", None),
            P(None, "seq", None),
            P("seq"),
            P("seq", "tp"),
            P("seq", "tp"),
            P("seq", "tp"),
            P("seq", "tp"),
            P("tp", "seq"),
            P("seq"),
            P("seq", "tp"),
            P("seq", "tp"),
            P("tp", "seq"),
        ),
        check_vma=False,
    )
```

time: 2470 us -> 688 us (0.28)
  waiting for transfers between devices: 2050 us -> 262 us
  Pallas kernels: 0 us -> 203 us
  blocking collectives: 80.8 us -> 0 us
  starting transfers between devices: 84.9 us -> 28.7 us
  matrix products: 132 us -> 103 us
  other arithmetic: 62.5 us -> 36.2 us
    reduce_scatter x8 -> x5, waiting for transfers between devices: 930 us -> 4.11 us  [scattered(): lax.psum_scatter(grad.astype(BF), 'seq', axis_index_groups=rings, scatter...]
    ppermute x14 -> x21, waiting for transfers between devices: 560 us -> 181 us  [the longest x6 114 us: shifted(): return lax.ppermute(block, 'seq', route)]
    psum x3 -> x0, waiting for transfers between devices: 243 us -> none  [the longest x1 101 us: on_device(): lax.psum(jnp.dot(hidden, full_down, preferred_element_type=jnp.float32),...]
    all_gather x8 -> x5, waiting for transfers between devices: 311 us -> 77.1 us  [gathered(): lax.all_gather(both, 'seq', axis_index_groups=rings, axis=0, tiled=True)]
    pallas_call x0 -> x4, Pallas kernels: none -> 203 us  [the longest x1 82 us: last_stage(): pl.pallas_call(last_kernel, name='last', out_shape=(jax.ShapeDtypeStruct(...]
    ppermute x14 -> x21, starting transfers between devices: 83.4 us -> 27.9 us  [the longest x6 10.6 us: shifted(): return lax.ppermute(block, 'seq', route)]
    all_gather x2 -> x0, blocking collectives: 42.4 us -> none  [the longest x1 22.4 us: on_device(): lax.all_gather(attn_gain, 'seq', axis=0, tiled=True)]
    unnamed x1 -> x0, blocking collectives: 38.5 us -> none
  transfers between devices with their start and end apart: 33 -> 31, of which waited for: 31 -> 19; matrix products, arithmetic and copies ran while one was open for 5% -> 19% of each run, Pallas kernels for 0% -> 30%
where the time goes in v1:
time: 688 us; the launch traced here: 683 us
  waiting for transfers between devices  262 us (38%)
  Pallas kernels  203 us (30%)
  matrix products  103 us (15%)
  other arithmetic  36.2 us (5%)
  local copies, waits for them, and re-layouts  32 us (5%)
  starting transfers between devices  28.7 us (4%)
  between operations  16.9 us (2%)
    ppermute x6, waiting for transfers between devices, shifted(): return lax.ppermute(block, 'seq', route)  114 us
    dot_general x31, matrix products, product(): return jnp.einsum(spec, left, right, preferred_element_type=F32)  103 us
    pallas_call x1, Pallas kernels, last_stage(): pl.pallas_call(last_kernel, name='last', out_shape=(jax.ShapeDtypeStruct(...  82 us
    all_gather x5, waiting for transfers between devices, gathered(): lax.all_gather(both, 'seq', axis_index_groups=rings, axis=0, tiled=True)  77.1 us
    pallas_call x1, Pallas kernels, turn_stage(): pl.pallas_call(turn_kernel, name='turn', out_shape=(jax.ShapeDtypeStruct(...  45.7 us
    pallas_call x1, Pallas kernels, middle_stage(): pl.pallas_call(middle_kernel, name='middle', out_shape=(jax.ShapeDtypeStr...  44.9 us
    ppermute x5, waiting for transfers between devices, gathered(): lax.ppermute(jnp.concatenate([m[1] for m in mine], axis=1), 'seq', pairs)  33.6 us
    pallas_call x1, Pallas kernels, entry(): pl.pallas_call(entry_kernel, name='entry', out_shape=(jax.ShapeDtypeStruc...  30.7 us
  transfers between devices with their start and end apart: 31, of which 19 were waited for; matrix products, arithmetic and copies ran while one was open for 19% of the time, Pallas kernels for 30%

profile of v1, /device:TPU:0, one launch (start us, length us, event | category | flops | bytes accessed | tf_op | source)
XLA Modules:
  0.0 682.9 jit_solution(14474865893378873578)
XLA Ops:
  11.5 5.4 collective-permute-done.3
  20.9 5.7 collective-permute-done.5
  30.4 10.5 %collective-permute-done.10 = bf16[256,864]{0,1:T(8,128)(2,1)S(1)} collective-permute-done((bf16[256,864]{0,1:T(8,128)(2,1)S(1)}, bf16[256,864]{0,1:T(8,128)(2,1)S(1)}, u32[]{:S(2)}, u32[]{:S(2)}) %collective-permute-start.10) | collective-permute-done | bytes 442400 | tf_op jit(solution)/shard_map/ppermute | solution.py:539
  40.9 6.9 %collective-permute-done.4 = bf16[256,864]{0,1:T(8,128)(2,1)S(1)} collective-permute-done((bf16[256,864]{0,1:T(8,128)(2,1)S(1)}, bf16[256,864]{0,1:T(8,128)(2,1)S(1)}, u32[]{:S(2)}, u32[]{:S(2)}) %collective-permute-start.4) | collective-permute-done | bytes 442400 | tf_op jit(solution)/shard_map/ppermute | solution.py:539
  53.5 5.1 collective-permute-done.9
  59.5 7.1 %collective-permute-done = bf16[128,2048]{1,0:T(8,128)(2,1)} collective-permute-done((bf16[128,2048]{1,0:T(8,128)(2,1)S(1)}, bf16[128,2048]{1,0:T(8,128)(2,1)}, u32[]{:S(2)}, u32[]{:S(2)}) %collective-permute-start) | collective-permute-done | bytes 524320 | tf_op jit(solution)/shard_map/ppermute | solution.py:610
  71.1 30.7 %entry.1 = (f32[128,2048]{1,0:T(8,128)}, f32[128,1]{1,0:T(8,128)}, f32[8,2048]{1,0:T(8,128)}, bf16[2,2,2,128,2048]{4,3,2,1,0:T(8,128)(2,1)}) custom-call(bf16[128,2048]{1,0:T(8,128)(2,1)} %dynamic-slice_bitcast_fusion.rows_ref, f32[8,256]{1,0:T(8,128)} %convert_element_type.156.gain_ref), custom_call_target="tpu_custom_call" | custom-call | tf_op jit(solution)/shard_map/entry/pallas_call | solution.py:262
  113.4 6.1 fusion.76
  119.5 5.2 fusion.77
  125.5 54.2 %all-gather.8.cloned.1.call-done = bf16[2048,864]{0,1:T(8,128)(2,1)} async-done(((bf16[512,864]{0,1:T(8,128)(2,1)}), bf16[2048,864]{0,1:T(8,128)(2,1)}) %all-gather.8.cloned.1.call-update) | async-done | bytes 3538960 | tf_op jit(solution)/shard_map/all_gather | solution.py:543
  179.6 4.8 fusion.23
  193.1 12.0 %collective-permute-done.6 = bf16[2,256,432]{1,2,0:T(8,128)(2,1)S(1)} collective-permute-done((bf16[2,256,432]{1,2,0:T(8,128)(2,1)S(1)}, bf16[2,256,432]{1,2,0:T(8,128)(2,1)S(1)}, u32[]{:S(2)}, u32[]{:S(2)}) %collective-permute-start.6) | collective-permute-done | bytes 442400 | tf_op jit(solution)/shard_map/ppermute | solution.py:481
  205.1 19.0 %collective-permute-done.7 = bf16[2,256,432]{1,2,0:T(8,128)(2,1)S(1)} collective-permute-done((bf16[2,256,432]{1,2,0:T(8,128)(2,1)S(1)}, bf16[2,256,432]{1,2,0:T(8,128)(2,1)S(1)}, u32[]{:S(2)}, u32[]{:S(2)}) %collective-permute-start.7) | collective-permute-done | bytes 442400 | tf_op jit(solution)/shard_map/ppermute | solution.py:481
  224.1 18.0 %collective-permute-done.8 = bf16[2,256,432]{1,2,0:T(8,128)(2,1)S(1)} collective-permute-done((bf16[2,256,432]{1,2,0:T(8,128)(2,1)S(1)}, bf16[2,256,432]{1,2,0:T(8,128)(2,1)S(1)}, u32[]{:S(2)}, u32[]{:S(2)}) %collective-permute-start.8) | collective-permute-done | bytes 442400 | tf_op jit(solution)/shard_map/ppermute | solution.py:481
  250.5 6.2 convolution_convert_fusion.1
  256.7 44.9 %middle.1 = (f32[128,2048]{1,0:T(8,128)}, f32[128,2048]{1,0:T(8,128)}, f32[128,1]{1,0:T(8,128)}, bf16[2,2,2,128,2048]{4,3,2,1,0:T(8,128)(2,1)}) custom-call(bf16[2,2,2,128,2048]{4,3,2,1,0:T(8,128)(2,1)} %bitcast.136, bf16[128,2048]{1,0:T(8,128)(2,1)} %dynamic-slice_bitcast_fusion.rows_ref, f32[8,2048]{1,0:T(8,128)} %get-tuple-element.25.gains_ref), custom_call_target="tpu_custom_call" | custom-call | tf_op jit(solution)/shard_map/middle/pallas_call | solution.py:314
  301.6 23.0 %all-gather.14.cloned.1.call-done = bf16[2048,864]{0,1:T(8,128)(2,1)} async-done(((bf16[512,864]{0,1:T(8,128)(2,1)}), bf16[2048,864]{0,1:T(8,128)(2,1)}) %all-gather.14.cloned.1.call-update) | async-done | bytes 3538960 | tf_op jit(solution)/shard_map/all_gather | solution.py:543
  324.6 4.9 fusion.9
  330.1 4.2 multiply_convert_fusion.2
  339.9 8.1 %convolution_convert_fusion.2 = bf16[1024,2048]{1,0:T(8,128)(2,1)} fusion(bf16[2048,864]{0,1:T(8,128)(2,1)} %all-gather.14.cloned.1.call-done, bf16[1024,432]{0,1:T(8,128)(2,1)S(1)} %copy-done.74, bf16[1024,432]{0,1:T(8,128)(2,1)S(1)} %copy-done.73), kind=kOutput, calls=%fused_computation.4 | convolution fusion | flops 3629514752 | bytes 9502720 | tf_op jit(solution)/shard_map/tn,dn->td/dot_general | solution.py:475
  348.0 45.7 %turn.1 = (f32[128,2048]{1,0:T(8,128)}, bf16[2,2,2,128,2048]{4,3,2,1,0:T(8,128)(2,1)}) custom-call(bf16[2,2,2,128,2048]{4,3,2,1,0:T(8,128)(2,1)} %bitcast.140, bf16[128,2048]{1,0:T(8,128)(2,1)} %copy-done.24, f32[8,2048]{1,0:T(8,128)} %get-tuple-element.25.gains_ref, f32[128,2048]{1,0:T(8,128)} %get-tuple-element.27.normed_ref, ...), custom_call_target="tpu_custom_call" | custom-call | tf_op jit(solution)/shard_map/turn/pallas_call | solution.py:360
  393.7 5.5 convolution_convert_fusion.6
  399.3 6.4 fusion.64
  410.1 8.3 %convolution_convert_fusion.4 = bf16[2048,864]{0,1:T(8,128)(2,1)} fusion(bf16[1024,2048]{1,0:T(8,128)(2,1)} %bitcast.165, bf16[1024,432]{0,1:T(8,128)(2,1)} %get-tuple-element.74, bf16[1024,432]{0,1:T(8,128)(2,1)} %get-tuple-element.73), kind=kOutput, calls=%fused_computation.6 | convolution fusion | flops 3629187072 | bytes 9502720 | tf_op jit(solution)/shard_map/td,tn->dn/dot_general | solution.py:475
  430.0 13.1 %collective-permute-done.11 = bf16[2,256,432]{1,2,0:T(8,128)(2,1)S(1)} collective-permute-done((bf16[2,256,432]{1,2,0:T(8,128)(2,1)S(1)}, bf16[2,256,432]{1,2,0:T(8,128)(2,1)S(1)}, u32[]{:S(2)}, u32[]{:S(2)}) %collective-permute-start.11) | collective-permute-done | bytes 442400 | tf_op jit(solution)/shard_map/ppermute | solution.py:481
  443.1 52.1 %collective-permute-done.12 = bf16[2,256,432]{1,2,0:T(8,128)(2,1)S(1)} collective-permute-done((bf16[2,256,432]{1,2,0:T(8,128)(2,1)S(1)}, bf16[2,256,432]{1,2,0:T(8,128)(2,1)S(1)}, u32[]{:S(2)}, u32[]{:S(2)}) %collective-permute-start.12) | collective-permute-done | bytes 442400 | tf_op jit(solution)/shard_map/ppermute | solution.py:481
  505.3 7.5 %convolution_convert_fusion.3 = bf16[2048,944]{0,1:T(8,128)(2,1)} fusion(bf16[1024,2048]{1,0:T(8,128)(2,1)S(1)} %bitcast.163, bf16[1024,432]{0,1:T(8,128)(2,1)S(1)} %bitcast.149, bf16[1024,256]{0,1:T(8,128)(2,1)S(1)} %copy-done.53, bf16[1024,256]{0,1:T(8,128)(2,1)S(1)} %copy-done.52), kind=kOutput, calls=%fused_computation.5 | convolution fusion | flops 3967156224 | bytes 9994240 | tf_op jit(solution)/shard_map/td,tn->dn/dot_general | solution.py:475
  515.4 5.7 convolution_convert_fusion
  526.0 6.0 add_convert_fusion
  532.0 82.0 %last.1 = (f32[2,2,128,2048]{3,2,1,0:T(8,128)}, bf16[2,2,128,2048]{3,2,1,0:T(8,128)(2,1)}) custom-call(bf16[2,2,2,128,2048]{4,3,2,1,0:T(8,128)(2,1)} %bitcast.119, bf16[2,2,2,128,2048]{4,3,2,1,0:T(8,128)(2,1)} %bitcast.141, f32[8,2048]{1,0:T(8,128)} %get-tuple-element.25.gains_ref, f32[128,2048]{1,0:T(8,128)} %get-tuple-element.30.normed_ref, ...), custom_call_target="tpu_custom_call" | custom-call | tf_op jit(solution)/shard_map/last/pallas_call | solution.py:435
  634.1 7.7 %collective-permute-done.16 = bf16[256,864]{0,1:T(8,128)(2,1)S(1)} collective-permute-done((bf16[256,864]{0,1:T(8,128)(2,1)S(1)}, bf16[256,864]{0,1:T(8,128)(2,1)S(1)}, u32[]{:S(2)}, u32[]{:S(2)}) %collective-permute-start.16) | collective-permute-done | bytes 442400 | tf_op jit(solution)/shard_map/ppermute | solution.py:680
  650.9 8.9 %collective-permute-done.14 = bf16[256,944]{0,1:T(8,128)(2,1)S(1)} collective-permute-done((bf16[256,944]{0,1:T(8,128)(2,1)S(1)}, bf16[256,944]{0,1:T(8,128)(2,1)S(1)}, u32[]{:S(2)}, u32[]{:S(2)}) %collective-permute-start.14) | collective-permute-done | bytes 483360 | tf_op jit(solution)/shard_map/ppermute | solution.py:680
  (323 shorter events, 135.2 us)
Async XLA Ops:
  7.2 106.2 %all-gather.6.cloned.1.call-start = ((), (), s32[]{:S(2)}) async-start(), calls=%async_computation.5 | async-start | bytes 2211840 | tf_op jit(solution)/shard_map/all_gather | solution.py:543
  8.5 8.5 %collective-permute-start.3 = (bf16[256,432]{0,1:T(8,128)(2,1)S(1)}, bf16[256,432]{0,1:T(8,128)(2,1)S(1)}, u32[]{:S(2)}, u32[]{:S(2)}) collective-permute-start(bf16[256,432]{0,1:T(8,128)(2,1)S(1)} %broadcast_select_fusion.36), channel_id=1, source_target_pairs={{0,4},{4,0},{8,12},{12,8},{16,20},{20,16},{24,28},{28,24},{1,5},{5... | collective-permute-start | bytes 663560 | tf_op jit(solution)/shard_map/ppermute | solution.py:539
  18.9 100.6 %all-gather.10.cloned.1.call-start = ((), (), s32[]{:S(2)}) async-start(), calls=%async_computation.7 | async-start | bytes 2621440 | tf_op jit(solution)/shard_map/all_gather | solution.py:543
  19.0 7.5 %collective-permute-start.5 = (bf16[256,512]{1,0:T(8,128)(2,1)S(1)}, bf16[256,512]{1,0:T(8,128)(2,1)S(1)}, u32[]{:S(2)}, u32[]{:S(2)}) collective-permute-start(bf16[256,512]{1,0:T(8,128)(2,1)S(1)} %pad_maximum_fusion.22), channel_id=1, source_target_pairs={{0,4},{4,0},{8,12},{12,8},{16,20},{20,16},{24,28},{28,24},{1,5},{5... | collective-permute-start | bytes 786440 | tf_op jit(solution)/shard_map/ppermute | solution.py:539
  27.5 152.1 %all-gather.8.cloned.1.call-start = ((), (), s32[]{:S(2)}) async-start(), calls=%async_computation.6 | async-start | bytes 4423680 | tf_op jit(solution)/shard_map/all_gather | solution.py:543
  27.8 13.1 %collective-permute-start.10 = (bf16[256,864]{0,1:T(8,128)(2,1)S(1)}, bf16[256,864]{0,1:T(8,128)(2,1)S(1)}, u32[]{:S(2)}, u32[]{:S(2)}) collective-permute-start(bf16[256,864]{0,1:T(8,128)(2,1)S(1)} %pad_maximum_fusion.20), channel_id=1, source_target_pairs={{0,4},{4,0},{8,12},{12,8},{16,20},{20,16},{24,28},{28,24},{1,5},{5... | collective-permute-start | bytes 1327112 | tf_op jit(solution)/shard_map/ppermute | solution.py:539
  29.4 18.4 %collective-permute-start.4 = (bf16[256,864]{0,1:T(8,128)(2,1)S(1)}, bf16[256,864]{0,1:T(8,128)(2,1)S(1)}, u32[]{:S(2)}, u32[]{:S(2)}) collective-permute-start(bf16[256,864]{0,1:T(8,128)(2,1)S(1)} %pad_maximum_fusion.17), channel_id=1, source_target_pairs={{0,4},{4,0},{8,12},{12,8},{16,20},{20,16},{24,28},{28,24},{1,5},{5... | collective-permute-start | bytes 1327112 | tf_op jit(solution)/shard_map/ppermute | solution.py:539
  50.1 200.4 %all-gather.12.cloned.1.call-start = ((), (), s32[]{:S(2)}) async-start(), calls=%async_computation.8 | async-start | bytes 2211840 | tf_op jit(solution)/shard_map/all_gather | solution.py:543
  50.2 8.4 %collective-permute-start.9 = (bf16[256,432]{0,1:T(8,128)(2,1)S(1)}, bf16[256,432]{0,1:T(8,128)(2,1)S(1)}, u32[]{:S(2)}, u32[]{:S(2)}) collective-permute-start(bf16[256,432]{0,1:T(8,128)(2,1)S(1)} %broadcast_select_fusion.28), channel_id=1, source_target_pairs={{0,4},{4,0},{8,12},{12,8},{16,20},{20,16},{24,28},{28,24},{1,5},{5... | collective-permute-start | bytes 663560 | tf_op jit(solution)/shard_map/ppermute | solution.py:539
  52.6 14.0 %collective-permute-start = (bf16[128,2048]{1,0:T(8,128)(2,1)S(1)}, bf16[128,2048]{1,0:T(8,128)(2,1)}, u32[]{:S(2)}, u32[]{:S(2)}) collective-permute-start(bf16[128,2048]{1,0:T(8,128)(2,1)S(1)} %dynamic-slice_bitcast_fusion.1.cot_ref), channel_id=1, source_target_pairs={{0,4},{4,0},{8,12},{12,8},{16,20},{20,16},{24,28},{28,24},{1,5},{5... | collective-permute-start | bytes 1572872 | tf_op jit(solution)/shard_map/ppermute | solution.py:610
  59.5 265.1 %all-gather.14.cloned.1.call-start = ((), (), s32[]{:S(2)}) async-start(), calls=%async_computation.9 | async-start | bytes 4423680 | tf_op jit(solution)/shard_map/all_gather | solution.py:543
  66.6 35.2 %collective-permute-start.1 = (bf16[128,2048]{1,0:T(8,128)(2,1)}, bf16[128,2048]{1,0:T(8,128)(2,1)S(1)}, u32[]{:S(2)}, u32[]{:S(2)}) collective-permute-start(bf16[128,2048]{1,0:T(8,128)(2,1)} %collective-permute-done), channel_id=1, source_target_pairs={{0,2},{1,3},{2,0},{3,1},{4,6},{5,7},{6,4},{7,5},{8,10},{9,11},{10,... | collective-permute-start | bytes 1572872 | tf_op jit(solution)/shard_map/ppermute | solution.py:611
  104.0 3.2 collective-permute-start.2
  104.4 137.8 %copy-start.54 = (f32[512]{0:T(512)}, f32[512]{0:T(512)S(1)}, u32[]{:S(2)}) copy-start(f32[512]{0:T(512)S(1)} %multiply_exponential_fusion.1) | copy-start | bytes 6148
  107.0 507.1 %reduce-scatter.14.cloned.1.call-start = ((), (), s32[]{:S(2)}) async-start(), calls=%async_computation.14 | async-start | bytes 2211840 | tf_op jit(solution)/shard_map/reduce_scatter | solution.py:623
  184.9 20.2 %collective-permute-start.6 = (bf16[2,256,432]{1,2,0:T(8,128)(2,1)S(1)}, bf16[2,256,432]{1,2,0:T(8,128)(2,1)S(1)}, u32[]{:S(2)}, u32[]{:S(2)}) collective-permute-start(bf16[2,256,432]{1,2,0:T(8,128)(2,1)S(1)} %convolution_convert_fusion.9), channel_id=1, source_target_pairs={{0,8},{4,12},{8,16},{12,20},{16,24},{20,28},{1,9},{5,13},{9,17},{1... | collective-permute-start | bytes 1327112 | tf_op jit(solution)/shard_map/ppermute | solution.py:481
  186.3 37.8 %collective-permute-start.7 = (bf16[2,256,432]{1,2,0:T(8,128)(2,1)S(1)}, bf16[2,256,432]{1,2,0:T(8,128)(2,1)S(1)}, u32[]{:S(2)}, u32[]{:S(2)}) collective-permute-start(bf16[2,256,432]{1,2,0:T(8,128)(2,1)S(1)} %convolution_convert_fusion.9), channel_id=1, source_target_pairs={{0,16},{4,20},{8,24},{12,28},{1,17},{5,21},{9,25},{13,29},{2,18},{... | collective-permute-start | bytes 1327112 | tf_op jit(solution)/shard_map/ppermute | solution.py:481
  190.0 52.0 %collective-permute-start.8 = (bf16[2,256,432]{1,2,0:T(8,128)(2,1)S(1)}, bf16[2,256,432]{1,2,0:T(8,128)(2,1)S(1)}, u32[]{:S(2)}, u32[]{:S(2)}) collective-permute-start(bf16[2,256,432]{1,2,0:T(8,128)(2,1)S(1)} %convolution_convert_fusion.9), channel_id=1, source_target_pairs={{0,24},{4,28},{1,25},{5,29},{2,26},{6,30},{3,27},{7,31}} | collective-permute-start | bytes 1327112 | tf_op jit(solution)/shard_map/ppermute | solution.py:481
  338.5 277.3 %reduce-scatter.12.cloned.1.call-start = ((), (), s32[]{:S(2)}) async-start(), calls=%async_computation.13 | async-start | bytes 2211840 | tf_op jit(solution)/shard_map/reduce_scatter | solution.py:623
  399.2 219.3 %reduce-scatter.8.cloned.1.call-start = ((), (), s32[]{:S(2)}) async-start(), calls=%async_computation.11 | async-start | bytes 2211840 | tf_op jit(solution)/shard_map/reduce_scatter | solution.py:623
  409.9 219.2 %reduce-scatter.10.cloned.1.call-start = ((), (), s32[]{:S(2)}) async-start(), calls=%async_computation.12 | async-start | bytes 4423680 | tf_op jit(solution)/shard_map/reduce_scatter | solution.py:623
  418.5 227.6 %reduce-scatter.6.cloned.1.call-start = ((), (), s32[]{:S(2)}) async-start(), calls=%async_computation.10 | async-start | bytes 4833280 | tf_op jit(solution)/shard_map/reduce_scatter | solution.py:623
  421.8 21.3 %collective-permute-start.11 = (bf16[2,256,432]{1,2,0:T(8,128)(2,1)S(1)}, bf16[2,256,432]{1,2,0:T(8,128)(2,1)S(1)}, u32[]{:S(2)}, u32[]{:S(2)}) collective-permute-start(bf16[2,256,432]{1,2,0:T(8,128)(2,1)S(1)} %convolution_convert_fusion.8), channel_id=1, source_target_pairs={{8,0},{12,4},{16,8},{20,12},{24,16},{28,20},{9,1},{13,5},{17,9},{2... | collective-permute-start | bytes 1327112 | tf_op jit(solution)/shard_map/ppermute | solution.py:481
  423.3 71.9 %collective-permute-start.12 = (bf16[2,256,432]{1,2,0:T(8,128)(2,1)S(1)}, bf16[2,256,432]{1,2,0:T(8,128)(2,1)S(1)}, u32[]{:S(2)}, u32[]{:S(2)}) collective-permute-start(bf16[2,256,432]{1,2,0:T(8,128)(2,1)S(1)} %convolution_convert_fusion.8), channel_id=1, source_target_pairs={{16,0},{20,4},{24,8},{28,12},{17,1},{21,5},{25,9},{29,13},{18,2},{... | collective-permute-start | bytes 1327112 | tf_op jit(solution)/shard_map/ppermute | solution.py:481
  424.6 70.6 %collective-permute-start.13 = (bf16[2,256,432]{1,2,0:T(8,128)(2,1)S(1)}, bf16[2,256,432]{1,2,0:T(8,128)(2,1)S(1)}, u32[]{:S(2)}, u32[]{:S(2)}) collective-permute-start(bf16[2,256,432]{1,2,0:T(8,128)(2,1)S(1)} %convolution_convert_fusion.8), channel_id=1, source_target_pairs={{24,0},{28,4},{25,1},{29,5},{26,2},{30,6},{27,3},{31,7}} | collective-permute-start | bytes 1327112 | tf_op jit(solution)/shard_map/ppermute | solution.py:481
  615.2 8.4 %collective-permute-start.20 = (bf16[256,432]{0,1:T(8,128)(2,1)S(1)}, bf16[256,432]{0,1:T(8,128)(2,1)S(1)}, u32[]{:S(2)}, u32[]{:S(2)}) collective-permute-start(bf16[256,432]{0,1:T(8,128)(2,1)S(1)} %broadcast_select_fusion.12), channel_id=1, source_target_pairs={{0,4},{4,0},{8,12},{12,8},{16,20},{20,16},{24,28},{28,24},{1,5},{5... | collective-permute-start | bytes 663560 | tf_op jit(solution)/shard_map/ppermute | solution.py:680
  616.9 11.4 %collective-permute-start.19 = (bf16[256,432]{0,1:T(8,128)(2,1)S(1)}, bf16[256,432]{0,1:T(8,128)(2,1)S(1)}, u32[]{:S(2)}, u32[]{:S(2)}) collective-permute-start(bf16[256,432]{0,1:T(8,128)(2,1)S(1)} %broadcast_select_fusion.16), channel_id=1, source_target_pairs={{0,4},{4,0},{8,12},{12,8},{16,20},{20,16},{24,28},{28,24},{1,5},{5... | collective-permute-start | bytes 663560 | tf_op jit(solution)/shard_map/ppermute | solution.py:680
  619.6 13.4 %collective-permute-start.15 = (bf16[256,432]{0,1:T(8,128)(2,1)S(1)}, bf16[256,432]{0,1:T(8,128)(2,1)S(1)}, u32[]{:S(2)}, u32[]{:S(2)}) collective-permute-start(bf16[256,432]{0,1:T(8,128)(2,1)S(1)} %broadcast_select_fusion.20), channel_id=1, source_target_pairs={{0,4},{4,0},{8,12},{12,8},{16,20},{20,16},{24,28},{28,24},{1,5},{5... | collective-permute-start | bytes 663560 | tf_op jit(solution)/shard_map/ppermute | solution.py:680
  630.3 11.5 %collective-permute-start.16 = (bf16[256,864]{0,1:T(8,128)(2,1)S(1)}, bf16[256,864]{0,1:T(8,128)(2,1)S(1)}, u32[]{:S(2)}, u32[]{:S(2)}) collective-permute-start(bf16[256,864]{0,1:T(8,128)(2,1)S(1)} %broadcast_select_fusion.2), channel_id=1, source_target_pairs={{0,4},{4,0},{8,12},{12,8},{16,20},{20,16},{24,28},{28,24},{1,5},{5... | collective-permute-start | bytes 1327112 | tf_op jit(solution)/shard_map/ppermute | solution.py:680
  647.3 12.5 %collective-permute-start.14 = (bf16[256,944]{0,1:T(8,128)(2,1)S(1)}, bf16[256,944]{0,1:T(8,128)(2,1)S(1)}, u32[]{:S(2)}, u32[]{:S(2)}) collective-permute-start(bf16[256,944]{0,1:T(8,128)(2,1)S(1)} %broadcast_select_fusion), channel_id=1, source_target_pairs={{0,4},{4,0},{8,12},{12,8},{16,20},{20,16},{24,28},{28,24},{1,5},{5... | collective-permute-start | bytes 1449992 | tf_op jit(solution)/shard_map/ppermute | solution.py:680
  662.3 1.7 collective-permute-start.17
  664.0 4.5 collective-permute-start.18
  (74 other events, 739.3 us)
Sparse Core Ops, SparseCore 0:
  19.0 41.7 all-gather.5
  62.9 45.8 all-gather.9
  111.0 68.5 all-gather.7
  181.6 61.6 all-gather.11
  245.3 79.2 all-gather.13
  338.6 37.0 reduce-scatter.13
  399.3 43.4 reduce-scatter.11
  445.7 56.2 reduce-scatter.7
  504.4 67.7 reduce-scatter.9
  574.3 71.7 reduce-scatter.5
